TPU v7x, 32 devices: a whole 2x2x4 slice. The times are simulated.
32 devices in a mesh: parts: 2 (over y), seq: 4 (over z), head: 2 (over x), rep: 2 (over core).
Axes of the slice: x: 2, y: 2, z: 4, core: 2. Of those that a mesh axis runs over, the one named last changes fastest.
Arguments:
- queries: bfloat16 [4, 1024, 2048], P(('parts', 'rep'), 'seq', 'head'), parts along dimension 0, may hold values from -6 to 6
- reflect_keys: bfloat16 [4, 1024, 2, 2048], P(('parts', 'rep'), 'seq', None, 'head'), parts along dimension 0, may hold values from -6 to 6
- reflect_values: bfloat16 [4, 1024, 2, 2048], P(('parts', 'rep'), 'seq', None, 'head'), parts along dimension 0, may hold values from -6 to 6
- reflect_beta: float32 [4, 1024, 2, 16], P(('parts', 'rep'), 'seq', None, 'head'), parts along dimension 0, may hold values from 0.2 to 2
- log_decay: float32 [4, 1024, 16], P(('parts', 'rep'), 'seq', 'head'), parts along dimension 0, may hold values from -2.5 to 0
- prompt_lengths: int32 [4, 6], P(('parts', 'rep')), parts along dimension 0, may hold values from 1 to 512, 1024 in all within a row
- norm_gain: float32 [128], replicated, may hold values from 0.1 to 1.9
- out_weight: bfloat16 [2048, 2048], P('head'), may hold values from -0.125 to 0.125
Outputs:
- layer_out: bfloat16 [4, 1024, 2048], P(('parts', 'rep'), ('seq', 'head')), parts along dimension 0
There are 2 independent parts, one for each index of `parts`. A program takes and returns all parts, laid end to end along the dimension named above; an argument that names none is the same for every part. Nothing has to cross between parts.
Inputs may be any that keep to these rules, and one draw needn't show every extreme that they name: `prompt_lengths`: the 6 prompts of a pack lie end to end from its first token and cover all 1024 tokens; the longest has exactly 512.
All inputs are finite; a program needn't handle non-finite values.
Results may differ from a plain program's by a relative error of at most 0.0095.
Values may be sent and summed in bfloat16 or wider, within the bound.
A program may use at most 64 MiB of HBM per device.

v0:
```python
import functools

import jax
import jax.numpy as jnp
from jax import lax
from jax.experimental import pallas as pl
from jax.experimental.pallas import tpu as pltpu
from jax.sharding import PartitionSpec as P

BLOCK = 64
HEADS_STEP = 4
STATE_GROUP = 2
PIECES = 4
MESH = pl.DeviceIdType.MESH

epsilon = 1e-06
f32 = jnp.float32
bf16 = jnp.bfloat16
highest = lax.Precision.HIGHEST


def mm(a, b, precision=None):
    return jnp.dot(a, b, preferred_element_type=f32, precision=precision)


def mm_nt(a, b):
    return lax.dot_general(a, b, (((1,), (1,)), ((), ())), preferred_element_type=f32)


def mm_tn(a, b):
    return lax.dot_general(a, b, (((0,), (0,)), ((), ())), preferred_element_type=f32)


def split(x):
    hi = x.astype(bf16)
    return hi, (x - hi.astype(f32)).astype(bf16)


def local_kernel(
    refl, blocks, len_ref, q_ref, k_ref, v_ref, beta_ref, gate_ref,
    oloc_ref, read_ref, add_ref, map_ref, rows_ref, kflat_ref,
):
    sub = refl * BLOCK
    width = k_ref.shape[2] // HEADS_STEP
    heads = gate_ref.shape[0]
    tokens = blocks * BLOCK
    step = pl.program_id(0)

    @pl.when(step == 0)
    def _():
        tok = lax.broadcasted_iota(jnp.int32, (tokens, sub), 0)
        lane = lax.broadcasted_iota(jnp.int32, (tokens, sub), 1)
        for b in range(blocks):
            rel = tok - b * BLOCK
            cum = jnp.where((rel >= 0) & (rel <= lane // refl), 1.0, 0.0).astype(f32)
            rows_ref[b, 0] = mm(gate_ref[...], cum, highest)
            total = jnp.zeros((heads, sub), f32)
            for j in range(refl):
                pick = jnp.where(rel * refl + j == lane, 1.0, 0.0).astype(f32)
                pick = jnp.where(rel >= 0, pick, 0.0)
                total += mm(beta_ref[j], pick, highest)
            rows_ref[b, 1] = total

    offset = lax.axis_index("seq") * tokens
    ends = []
    running = 0
    for d in range(len_ref.shape[1]):
        running = running + len_ref[0, d]
        ends.append(running)

    def segment(pos):
        total = jnp.zeros(pos.shape, jnp.int32)
        for end in ends:
            total += jnp.where(pos >= end, 1, 0)
        return total

    row_i = lax.broadcasted_iota(jnp.int32, (sub, sub), 0)
    col_i = lax.broadcasted_iota(jnp.int32, (sub, sub), 1)
    eye = row_i == col_i
    eye_f = jnp.where(eye, 1.0, 0.0).astype(f32)
    tok_i = lax.broadcasted_iota(jnp.int32, (BLOCK, sub), 0)
    tok_j = lax.broadcasted_iota(jnp.int32, (BLOCK, sub), 1)
    pick_tok = tok_j == tok_i * refl + refl - 1
    levels = []
    size = refl
    while size < sub:
        big = min(4 * size, sub)
        levels.append((row_i // big == col_i // big) & (row_i // size > col_i // size))
        size = big

    blocks_geo = []
    for b in range(blocks):
        start = offset + b * BLOCK
        seg_row = segment(start + lax.broadcasted_iota(jnp.int32, (1, sub), 1) // refl)
        seg_col = segment(start + lax.broadcasted_iota(jnp.int32, (sub, 1), 0) // refl)
        seg_tok = segment(start + lax.broadcasted_iota(jnp.int32, (BLOCK, 1), 0))
        before = jnp.where(start == 0, -1, 0)
        last_seg = 0
        for end in ends:
            before += jnp.where(start - 1 >= end, 1, 0)
            last_seg += jnp.where(start + BLOCK - 1 >= end, 1, 0)
        incl = (row_i >= col_i) & (seg_col == seg_row)
        read = (tok_j // refl <= tok_i) & (seg_tok == seg_row)
        blocks_geo.append(
            (incl, read, seg_row == before, seg_tok == before, seg_col == last_seg, last_seg == before)
        )

    pairs = [(h, b) for h in range(HEADS_STEP) for b in range(blocks)]

    def over(stage, *lists):
        return [stage(h, b, *args) for (h, b), *args in zip(pairs, *lists)]

    def cols(h):
        return slice(h * width, (h + 1) * width)

    def keys(h, b):
        return kflat_ref[b * sub : (b + 1) * sub, cols(h)]

    for h, b in pairs:
        kflat_ref[b * sub : (b + 1) * sub, cols(h)] = k_ref[
            b * BLOCK : (b + 1) * BLOCK, :, cols(h)
        ].reshape(sub, width)

    def row(kind, h, b):
        return rows_ref[b, kind, pl.ds(step * HEADS_STEP + h, 1), :]

    def column(values):
        return jnp.sum(jnp.where(eye, values, 0.0), axis=1, keepdims=True)

    def scales(h, b):
        gram = mm_nt(keys(h, b), keys(h, b))
        diag = jnp.where(eye, gram, 0.0)
        n_row = lax.rsqrt(jnp.sum(diag, axis=0, keepdims=True) + epsilon)
        n_col = lax.rsqrt(jnp.sum(diag, axis=1, keepdims=True) + epsilon)
        c_row = row(0, h, b)
        c_col = column(c_row)
        ratio = jnp.where(blocks_geo[b][0], jnp.exp(jnp.minimum(c_col - c_row, 0.0)), 0.0)
        low = jnp.where(eye, 0.0, (column(row(1, h, b)) * n_col) * ratio * gram * n_row)
        return low, n_row, n_col, c_col

    lows, n_rows, n_cols, c_cols = zip(*over(scales))
    invs = [eye_f - jnp.where(row_i // refl == col_i // refl, low, 0.0) for low in lows]
    for mask in levels:
        heads_b = [inv.astype(bf16) for inv in invs]
        nils = [
            mm(inv, jnp.where(mask, low, 0.0).astype(bf16)).astype(bf16)
            for inv, low in zip(heads_b, lows)
        ]
        both = [mm(nil, jnp.concatenate([nil, inv], axis=1)) for nil, inv in zip(nils, heads_b)]
        halves = [inv - pair[:, sub:] for inv, pair in zip(invs, both)]
        invs = [
            half + mm(pair[:, :sub].astype(bf16), half.astype(bf16))
            for half, pair in zip(halves, both)
        ]

    def residual(h, b, inv, low):
        inv_b = inv.astype(bf16)
        low_2 = jnp.concatenate(split(low), axis=1)
        return eye_f - inv_b.astype(f32) - mm(low_2, jnp.concatenate([inv_b, inv_b], axis=0))

    resids = over(residual, invs, lows)

    def refine(h, b, inv, resid):
        inv_b = inv.astype(bf16)
        return inv_b.astype(f32) + mm(inv_b, resid.astype(bf16))

    invs = over(refine, invs, resids)

    def write(h, b, inv, n_row):
        carry_row = jnp.where(blocks_geo[b][2], jnp.exp(row(0, h, b)), 0.0)
        by_beta = inv * row(1, h, b)
        tv = jnp.concatenate(split(by_beta), axis=1)
        tk = jnp.concatenate(split(by_beta * (carry_row * n_row)), axis=1)
        vb, kb = v_ref[b * BLOCK : (b + 1) * BLOCK, :, cols(h)].reshape(sub, width), keys(h, b)
        return jnp.concatenate(
            [mm(tv, jnp.concatenate([vb, vb], axis=0)), mm(tk, jnp.concatenate([kb, kb], axis=0))],
            axis=1,
        )

    writes = over(write, invs, n_rows)

    def block_step(h, b, wrote, n_col, c_col):
        c_end = row(0, h, b)[:, sub - 1 : sub]
        e_col = jnp.where(blocks_geo[b][4], jnp.exp(jnp.minimum(c_end - c_col, 0.0)), 0.0) * n_col
        kb = keys(h, b)
        moved = mm_tn(
            jnp.concatenate([kb, kb], axis=0), jnp.concatenate(split(wrote * e_col), axis=0)
        )
        carry_end = jnp.where(blocks_geo[b][5], jnp.exp(c_end), 0.0)
        return moved[:, :width], carry_end * eye_f - moved[:, width:]

    steps = over(block_step, writes, n_cols, c_cols)

    def read_weights(h, b, n_row):
        qb, c_row = q_ref[b * BLOCK : (b + 1) * BLOCK, cols(h)], row(0, h, b)
        qf = qb.astype(f32)
        nq = lax.rsqrt(jnp.sum(qf * qf, axis=1, keepdims=True) + epsilon) * width ** (-0.5)
        ct = jnp.sum(jnp.where(pick_tok, c_row, 0.0), axis=1, keepdims=True)
        ratio = jnp.where(blocks_geo[b][1], jnp.exp(jnp.minimum(ct - c_row, 0.0)), 0.0)
        carried = (jnp.where(blocks_geo[b][3], jnp.exp(ct), 0.0) * nq) * qf
        return (ratio * mm_nt(qb, keys(h, b)) * nq * n_row).astype(bf16), carried

    weights = over(read_weights, n_rows)

    def read(h, b, weight, wrote):
        got = mm(weight[0], wrote.astype(bf16))
        return got[:, :width], weight[1] - got[:, width:]

    reads = over(read, weights, writes)

    def emit(h, b, own, back):
        oloc_ref[step, b * BLOCK : (b + 1) * BLOCK, cols(h)] = own
        read_ref[step, b * BLOCK : (b + 1) * BLOCK, cols(h)] = back.astype(bf16)

    at = lambda h, b: h * blocks + b
    states = [jnp.concatenate(steps[at(h, 0)], axis=1) for h in range(HEADS_STEP)]
    for h in range(HEADS_STEP):
        emit(h, 0, *reads[at(h, 0)])
    for b in range(1, blocks):
        for h in range(HEADS_STEP):
            block_add, block_map = steps[at(h, b)]
            own, back = reads[at(h, b)]
            s_hi, s_lo = split(states[h])
            m_hi, m_lo = split(block_map)
            moved = mm(back.astype(bf16), s_hi)
            emit(h, b, own + moved[:, :width], moved[:, width:])
            grown = mm(
                jnp.concatenate([m_hi, m_lo], axis=1), jnp.concatenate([s_hi, s_hi], axis=0)
            ) + mm(m_hi, s_lo)
            states[h] = jnp.concatenate([grown[:, :width] + block_add, grown[:, width:]], axis=1)
    for h in range(HEADS_STEP):
        add_ref[step * HEADS_STEP + h] = states[h][:, :width]
        map_ref[step * HEADS_STEP + h] = states[h][:, width:]


def mixer_kernel(
    refl, blocks, len_ref, q_ref, k_ref, v_ref, beta_ref, gate_ref, gain_ref, weight_hbm, out_ref,
    rows_ref, kflat_ref, oloc_ref, read_ref, add_ref, map_ref,
    weight_ref, weight_sem, state_in, state_out, normed_ref, own_ref, part_out, part_in,
    state_send, state_recv, part_send, part_recv,
):
    heads, width = add_ref.shape[:2]
    step, steps = pl.program_id(0), heads // HEADS_STEP
    groups = heads // STATE_GROUP
    seq_count, head_count = lax.axis_size("seq"), lax.axis_size("head")
    seq_here, head_here = lax.axis_index("seq"), lax.axis_index("head")
    chunk = out_ref.shape[0]
    first, last = seq_here == 0, seq_here == seq_count - 1
    others = [lax.rem(head_here + d, head_count) for d in range(1, head_count)]
    load = pltpu.make_async_copy(weight_hbm, weight_ref, weight_sem)

    @pl.when(step == 0)
    def _():
        load.start()
        barrier = pltpu.get_barrier_semaphore()

        @pl.when(seq_here > 0)
        def _():
            pl.semaphore_signal(barrier, inc=1, device_id={"seq": seq_here - 1}, device_id_type=MESH)

        @pl.when(seq_here < seq_count - 1)
        def _():
            pl.semaphore_signal(barrier, inc=1, device_id={"seq": seq_here + 1}, device_id_type=MESH)

        for other in others:
            pl.semaphore_signal(barrier, inc=1, device_id={"head": other}, device_id_type=MESH)

    local_kernel(
        refl, blocks, len_ref, q_ref, k_ref, v_ref, beta_ref, gate_ref,
        oloc_ref, read_ref, add_ref, map_ref, rows_ref, kflat_ref,
    )

    @pl.when(step == 0)
    def _():
        expected = jnp.where(first, 0, 1) + jnp.where(last, 0, 1) + head_count - 1
        pl.semaphore_wait(pltpu.get_barrier_semaphore(), expected)

        @pl.when(first)
        def _():
            state_in[...] = jnp.zeros_like(state_in)

    def hop(g):
        part = pl.ds(g * STATE_GROUP, STATE_GROUP)
        return pltpu.make_async_remote_copy(
            src_ref=state_out.at[part],
            dst_ref=state_in.at[part],
            send_sem=state_send.at[g],
            recv_sem=state_recv.at[g],
            device_id={"seq": lax.rem(seq_here + 1, seq_count)},
            device_id_type=MESH,
        )

    @pl.when((seq_here == 0) & (seq_here < seq_count - 1))
    def _():
        for g in range(HEADS_STEP // STATE_GROUP):
            here = step * (HEADS_STEP // STATE_GROUP) + g
            for h in range(STATE_GROUP):
                state_out[here * STATE_GROUP + h] = add_ref[here * STATE_GROUP + h].astype(bf16)
            hop(here).start()

    @pl.when(step == steps - 1)
    def _():
        for g in range(groups):
            group = range(g * STATE_GROUP, (g + 1) * STATE_GROUP)

            @pl.when(seq_here > 0)
            def _():
                hop(g).wait_recv()

            @pl.when((seq_here > 0) & (seq_here < seq_count - 1))
            def _():
                for h in group:
                    state = state_in[h]
                    both = jnp.concatenate(split(map_ref[h]), axis=1)
                    grown = add_ref[h] + mm(both, jnp.concatenate([state, state], axis=0))
                    state_out[h] = grown.astype(bf16)
                hop(g).start()

            for h in group:
                cols = slice(h * width, (h + 1) * width)
                at, local = h // HEADS_STEP, slice(h % HEADS_STEP * width, (h % HEADS_STEP + 1) * width)
                out = oloc_ref[at, :, local] + mm(read_ref[at, :, local], state_in[h])
                scale = lax.rsqrt(jnp.mean(out * out, axis=-1, keepdims=True) + epsilon)
                normed_ref[:, cols] = (out * scale * gain_ref[...]).astype(bf16)

        load.wait()
        piece = weight_ref.shape[1] // PIECES
        copies = []
        for slot, other in enumerate(others):
            rows = normed_ref[pl.ds(pl.multiple_of(other * chunk, chunk), chunk), :]
            for p in range(PIECES):
                cols = pl.ds(p * piece, piece)
                part_out[slot, :, cols] = mm(rows, weight_ref[:, cols]).astype(bf16)
                copies.append(
                    pltpu.make_async_remote_copy(
                        src_ref=part_out.at[slot, :, cols],
                        dst_ref=part_in.at[slot, :, cols],
                        send_sem=part_send.at[slot, p],
                        recv_sem=part_recv.at[slot, p],
                        device_id={"head": other},
                        device_id_type=MESH,
                    )
                )
                copies[-1].start()
        rows = normed_ref[pl.ds(pl.multiple_of(head_here * chunk, chunk), chunk), :]
        for p in range(PIECES):
            cols = pl.ds(p * piece, piece)
            own_ref[:, cols] = mm(rows, weight_ref[:, cols])
        for p in range(PIECES):
            cols = pl.ds(p * piece, piece)
            total = own_ref[:, cols].astype(bf16).astype(f32)
            for slot in range(len(others)):
                copies[slot * PIECES + p].wait_recv()
                total += part_in[slot, :, cols].astype(f32)
            out_ref[:, cols] = total.astype(bf16)
        for copy in copies:
            copy.wait_send()

        @pl.when(seq_here < seq_count - 1)
        def _():
            for g in range(groups):
                hop(g).wait_send()


def body(queries, reflect_keys, reflect_values, reflect_beta, log_decay, prompt_lengths, norm_gain, out_weight):
    tokens, refl, wide = reflect_keys.shape[1:]
    heads = log_decay.shape[2]
    width = wide // heads
    blocks = tokens // BLOCK
    head_count = lax.axis_size("head")
    chunk, model = tokens // head_count, out_weight.shape[1]
    groups, steps, slots = heads // STATE_GROUP, heads // HEADS_STEP, max(head_count - 1, 1)
    wide_step = HEADS_STEP * width
    beta, gate = reflect_beta[0].transpose(1, 2, 0), log_decay[0].T
    whole = lambda shape: pl.BlockSpec(shape, lambda i: (0,) * len(shape))
    column = lambda rows: pl.BlockSpec((rows, wide_step), lambda i: (0, i))
    sub_column = pl.BlockSpec((tokens, refl, wide_step), lambda i: (0, 0, i))
    dma = pltpu.SemaphoreType.DMA
    out = pl.pallas_call(
        functools.partial(mixer_kernel, refl, blocks),
        grid=(steps,),
        in_specs=[
            pl.BlockSpec(memory_space=pltpu.SMEM),
            column(tokens), sub_column, sub_column,
            whole(beta.shape), whole(gate.shape), whole((1, width)),
            pl.BlockSpec(memory_space=pl.ANY),
        ],
        out_specs=whole((chunk, model)),
        out_shape=jax.ShapeDtypeStruct((chunk, model), bf16),
        scratch_shapes=[
            pltpu.VMEM((blocks, 2, heads, refl * BLOCK), f32),
            pltpu.VMEM((tokens * refl, wide_step), bf16),
            pltpu.VMEM((steps, tokens, wide_step), f32),
            pltpu.VMEM((steps, tokens, wide_step), bf16),
            pltpu.VMEM((heads, width, width), f32),
            pltpu.VMEM((heads, width, width), f32),
            pltpu.VMEM(out_weight.shape, bf16),
            dma,
            pltpu.VMEM((heads, width, width), bf16),
            pltpu.VMEM((heads, width, width), bf16),
            pltpu.VMEM((tokens, wide), bf16),
            pltpu.VMEM((chunk, model), f32),
            pltpu.VMEM((slots, chunk, model), bf16),
            pltpu.VMEM((slots, chunk, model), bf16),
            dma((groups,)), dma((groups,)), dma((slots, PIECES)), dma((slots, PIECES)),
        ],
        compiler_params=pltpu.CompilerParams(
            collective_id=0, has_side_effects=True, vmem_limit_bytes=56 * 2**20
        ),
    )(
        prompt_lengths,
        queries[0],
        reflect_keys[0],
        reflect_values[0],
        beta,
        gate,
        norm_gain[None],
        out_weight,
    )
    return out[None]


def solution(mesh):
    in_specs = (
        P(("parts", "rep"), "seq", "head"),
        P(("parts", "rep"), "seq", None, "head"),
        P(("parts", "rep"), "seq", None, "head"),
        P(("parts", "rep"), "seq", None, "head"),
        P(("parts", "rep"), "seq", "head"),
        P(("parts", "rep"), None),
        P(),
        P("head", None),
    )
    out_specs = P(("parts", "rep"), ("seq", "head"), None)
    return jax.shard_map(body, mesh=mesh, in_specs=in_specs, out_specs=out_specs, check_vma=False)
```

profile of v0, /device:TPU:28, one launch (start us, length us, event | category | flops | bytes accessed | tf_op | source)
XLA Modules:
  0.0 40.2 jit_solution(13024927323331304478)
XLA Ops:
  0.0 38.4 %shard_map.82 = bf16[128,2048]{1,0:T(8,128)(2,1)} custom-call(s32[1,6]{1,0:T(1,128)} %len_ref.1, bf16[256,1024]{1,0:T(8,128)(2,1)} %bitcast.14, bf16[256,2,1024]{2,1,0:T(2,128)(2,1)} %bitcast.12, bf16[256,2,1024]{2,1,0:T(2,128)(2,1)} %bitcast.13, f32[2,8,256]{2,1,0:T(8,128)} %bitcast.15, f32[8,256]{1,0:T(8,128)} %bitcast.16, f32[1,128]{1,0:T(1,128)} %bitcast.17, ...), custom_call_target="tpu_custom_call" | custom-call | tf_op jit(solution)/shard_map/pallas_call | solution.py:379
  38.4 1.9 %copy.10 = bf16[1,128,2048]{2,1,0:T(8,128)(2,1)} copy(bf16[1,128,2048]{2,1,0:T(8,128)(2,1)} %bitcast.11) | data formatting | bytes 1048576
where the time goes:
time: 40.4 us; the launch traced here: 40.2 us
  Pallas kernels  38.4 us (95%)
  local copies, waits for them, and re-layouts  1.88 us (5%)
    pallas_call x1, Pallas kernels, body(): pl.pallas_call(functools.partial(mixer_kernel, refl, blocks), grid=(steps...  38.4 us
    unnamed x1, local copies, waits for them, and re-layouts  1.88 us

commit v1 on v0

v1 whole, which is shorter than its diff:
```python
import functools

import jax
import jax.numpy as jnp
from jax import lax
from jax.experimental import pallas as pl
from jax.experimental.pallas import tpu as pltpu
from jax.sharding import PartitionSpec as P

BLOCK = 64
HEADS_STEP = 4
FINISH_GROUP = 2
PIECES = 4
MESH = pl.DeviceIdType.MESH

epsilon = 1e-06
f32 = jnp.float32
bf16 = jnp.bfloat16
highest = lax.Precision.HIGHEST


def mm(a, b, precision=None):
    return jnp.dot(a, b, preferred_element_type=f32, precision=precision)


def mm_nt(a, b):
    return lax.dot_general(a, b, (((1,), (1,)), ((), ())), preferred_element_type=f32)


def mm_tn(a, b):
    return lax.dot_general(a, b, (((0,), (0,)), ((), ())), preferred_element_type=f32)


def split(x):
    hi = x.astype(bf16)
    return hi, (x - hi.astype(f32)).astype(bf16)


def split3(x):
    hi = x.astype(bf16).astype(f32)
    mid = (x - hi).astype(bf16).astype(f32)
    return [hi, mid, x - hi - mid]


def sub_rows(x, pattern, blocks):
    rows = x.shape[0]
    zero = jnp.zeros_like(pattern)
    table = jnp.concatenate(
        [jnp.concatenate([pattern if c == r else zero for c in range(blocks)], axis=1) for r in range(blocks)],
        axis=0,
    )
    got = mm(jnp.concatenate(split3(x), axis=0).astype(bf16), table)
    return got[:rows] + got[rows : 2 * rows] + got[2 * rows :]


def mixer_kernel(
    refl, blocks, len_ref, q_hbm, k_hbm, v_hbm, beta_hbm, gate_hbm, gain_ref, weight_hbm, out_ref,
    q_ref, k_ref, v_ref, beta_ref, gate_ref, in_sem,
    rows_ref, scale_ref, kflat_ref, wrote_ref, prefix_ref, oloc_ref, read_ref, add_ref, map_ref,
    weight_ref, weight_sem, state_in, state_out, normed_ref, own_ref, part_out, part_in,
    state_send, state_recv, part_send, part_recv,
):
    heads, width = add_ref.shape[:2]
    steps = heads // HEADS_STEP
    wide = HEADS_STEP * width
    sub = refl * BLOCK
    tokens = blocks * BLOCK
    seq_count, head_count = lax.axis_size("seq"), lax.axis_size("head")
    seq_here, head_here = lax.axis_index("seq"), lax.axis_index("head")
    chunk = out_ref.shape[0]
    first, last = seq_here == 0, seq_here == seq_count - 1
    others = [lax.rem(head_here + d, head_count) for d in range(1, head_count)]

    def load(s, kind):
        span = pl.ds(pl.multiple_of(s * wide, wide), wide)
        src, dst = [
            (k_hbm.at[:, :, span], k_ref), (v_hbm.at[:, :, span], v_ref), (q_hbm.at[:, span], q_ref)
        ][kind]
        return pltpu.make_async_copy(src, dst.at[s], in_sem.at[s, kind])

    load_beta = pltpu.make_async_copy(beta_hbm, beta_ref, weight_sem.at[1])
    load_gate = pltpu.make_async_copy(gate_hbm, gate_ref, weight_sem.at[2])
    load_weight = pltpu.make_async_copy(weight_hbm, weight_ref, weight_sem.at[0])
    load_gate.start()
    load_beta.start()
    for s in range(steps):
        load(s, 0).start()
        load(s, 1).start()
    for s in range(steps):
        load(s, 2).start()
    load_weight.start()

    barrier = pltpu.get_barrier_semaphore()

    @pl.when(seq_here > 0)
    def _():
        pl.semaphore_signal(barrier, inc=1, device_id={"seq": seq_here - 1}, device_id_type=MESH)

    @pl.when(seq_here < seq_count - 1)
    def _():
        pl.semaphore_signal(barrier, inc=1, device_id={"seq": seq_here + 1}, device_id_type=MESH)

    for other in others:
        pl.semaphore_signal(barrier, inc=1, device_id={"head": other}, device_id_type=MESH)

    offset = seq_here * tokens
    ends = []
    running = 0
    for d in range(len_ref.shape[1]):
        running = running + len_ref[0, d]
        ends.append(running)

    def segment(pos):
        total = jnp.zeros(pos.shape, jnp.int32)
        for end in ends:
            total += jnp.where(pos >= end, 1, 0)
        return total

    row_i = lax.broadcasted_iota(jnp.int32, (sub, sub), 0)
    col_i = lax.broadcasted_iota(jnp.int32, (sub, sub), 1)
    eye = row_i == col_i
    eye_f = jnp.where(eye, 1.0, 0.0).astype(f32)
    tok_i = lax.broadcasted_iota(jnp.int32, (BLOCK, sub), 0)
    tok_j = lax.broadcasted_iota(jnp.int32, (BLOCK, sub), 1)
    pick_tok = tok_j == tok_i * refl + refl - 1
    levels = []
    size = refl
    while size < sub:
        big = min(4 * size, sub)
        levels.append((row_i // big == col_i // big) & (row_i // size > col_i // size))
        size = big

    load_gate.wait()
    load_beta.wait()
    table = sub_rows(gate_ref[...], jnp.where(tok_i <= tok_j // refl, 1.0, 0.0).astype(bf16), blocks)
    total = 0.0
    for j in range(refl):
        pick = jnp.where(tok_i * refl + j == tok_j, 1.0, 0.0).astype(bf16)
        total += sub_rows(beta_ref[j], pick, blocks)
    for b in range(blocks):
        rows_ref[b, 0] = table[:, b * sub : (b + 1) * sub]
        rows_ref[b, 1] = total[:, b * sub : (b + 1) * sub]

    def geometry(b):
        start = offset + b * BLOCK
        seg_row = segment(start + lax.broadcasted_iota(jnp.int32, (1, sub), 1) // refl)
        before = jnp.where(start == 0, -1, 0)
        last_seg = 0
        for end in ends:
            before += jnp.where(start - 1 >= end, 1, 0)
            last_seg += jnp.where(start + BLOCK - 1 >= end, 1, 0)
        return start, seg_row, before, last_seg

    pairs = [(h, b) for h in range(HEADS_STEP) for b in range(blocks)]

    def over(stage, *lists):
        return [stage(h, b, *args) for (h, b), *args in zip(pairs, *lists)]

    def cols(h):
        return slice(h * width, (h + 1) * width)

    def toks(b):
        return slice(b * BLOCK, (b + 1) * BLOCK)

    def column(values):
        return jnp.sum(jnp.where(eye, values, 0.0), axis=1, keepdims=True)

    def hop(h):
        return pltpu.make_async_remote_copy(
            src_ref=state_out.at[h],
            dst_ref=state_in.at[h],
            send_sem=state_send.at[h],
            recv_sem=state_recv.at[h],
            device_id={"seq": lax.rem(seq_here + 1, seq_count)},
            device_id_type=MESH,
        )

    def forward(h):
        hop(h).wait_recv()
        state = state_in[h]
        both = jnp.concatenate(split(map_ref[h]), axis=1)
        grown = add_ref[h] + mm(both, jnp.concatenate([state, state], axis=0))
        state_out[h] = grown.astype(bf16)
        hop(h).start()

    def near(s, b):
        def keys(h):
            return kflat_ref[s, b * sub : (b + 1) * sub, cols(h)]

        def row(kind, h):
            return rows_ref[b, kind, pl.ds(s * HEADS_STEP + h, 1), :]

        return keys, row

    def states_step(s, carry):
        load(s, 0).wait()
        load(s, 1).wait()
        keys = lambda h, b: near(s, b)[0](h)
        row = lambda kind, h, b: near(s, b)[1](kind, h)
        geo = []
        for b in range(blocks):
            start, seg_row, before, last_seg = geometry(b)
            seg_col = segment(start + lax.broadcasted_iota(jnp.int32, (sub, 1), 0) // refl)
            incl = (row_i >= col_i) & (seg_col == seg_row)
            geo.append((incl, seg_row == before, seg_col == last_seg, last_seg == before))

        for h, b in pairs:
            kflat_ref[s, b * sub : (b + 1) * sub, cols(h)] = k_ref[s, toks(b), :, cols(h)].reshape(sub, width)

        def scales(h, b):
            gram = mm_nt(keys(h, b), keys(h, b))
            diag = jnp.where(eye, gram, 0.0)
            n_row = lax.rsqrt(jnp.sum(diag, axis=0, keepdims=True) + epsilon)
            n_col = lax.rsqrt(jnp.sum(diag, axis=1, keepdims=True) + epsilon)
            scale_ref[b, pl.ds(s * HEADS_STEP + h, 1), :] = n_row
            c_row = row(0, h, b)
            c_col = column(c_row)
            ratio = jnp.where(geo[b][0], jnp.exp(jnp.minimum(c_col - c_row, 0.0)), 0.0)
            low = jnp.where(eye, 0.0, (column(row(1, h, b)) * n_col) * ratio * gram * n_row)
            return low, n_row, n_col, c_col

        lows, n_rows, n_cols, c_cols = zip(*over(scales))
        invs = [eye_f - jnp.where(row_i // refl == col_i // refl, low, 0.0) for low in lows]
        for mask in levels:
            heads_b = [inv.astype(bf16) for inv in invs]
            nils = [
                mm(inv, jnp.where(mask, low, 0.0).astype(bf16)).astype(bf16)
                for inv, low in zip(heads_b, lows)
            ]
            both = [mm(nil, jnp.concatenate([nil, inv], axis=1)) for nil, inv in zip(nils, heads_b)]
            halves = [inv - pair[:, sub:] for inv, pair in zip(invs, both)]
            invs = [
                half + mm(pair[:, :sub].astype(bf16), half.astype(bf16))
                for half, pair in zip(halves, both)
            ]

        def residual(h, b, inv, low):
            inv_b = inv.astype(bf16)
            low_2 = jnp.concatenate(split(low), axis=1)
            return eye_f - inv_b.astype(f32) - mm(low_2, jnp.concatenate([inv_b, inv_b], axis=0))

        resids = over(residual, invs, lows)

        def refine(h, b, inv, resid):
            inv_b = inv.astype(bf16)
            return inv_b.astype(f32) + mm(inv_b, resid.astype(bf16))

        invs = over(refine, invs, resids)

        def write(h, b, inv, n_row):
            carry_row = jnp.where(geo[b][1], jnp.exp(row(0, h, b)), 0.0)
            by_beta = inv * row(1, h, b)
            tv = jnp.concatenate(split(by_beta), axis=1)
            tk = jnp.concatenate(split(by_beta * (carry_row * n_row)), axis=1)
            vb, kb = v_ref[s, toks(b), :, cols(h)].reshape(sub, width), keys(h, b)
            return jnp.concatenate(
                [mm(tv, jnp.concatenate([vb, vb], axis=0)), mm(tk, jnp.concatenate([kb, kb], axis=0))],
                axis=1,
            )

        writes = over(write, invs, n_rows)

        def block_step(h, b, wrote, n_col, c_col):
            wrote_ref[s * HEADS_STEP + h, b] = wrote.astype(bf16)
            c_end = row(0, h, b)[:, sub - 1 : sub]
            e_col = jnp.where(geo[b][2], jnp.exp(jnp.minimum(c_end - c_col, 0.0)), 0.0) * n_col
            kb = keys(h, b)
            moved = mm_tn(
                jnp.concatenate([kb, kb], axis=0), jnp.concatenate(split(wrote * e_col), axis=0)
            )
            carry_end = jnp.where(geo[b][3], jnp.exp(c_end), 0.0)
            return moved[:, :width], carry_end * eye_f - moved[:, width:]

        made = over(block_step, writes, n_cols, c_cols)
        states = [jnp.concatenate(made[h * blocks], axis=1) for h in range(HEADS_STEP)]
        for b in range(1, blocks):
            for h in range(HEADS_STEP):
                block_add, block_map = made[h * blocks + b]
                s_hi = states[h].astype(bf16)
                prefix_ref[s * HEADS_STEP + h, b - 1] = s_hi
                grown = mm(
                    jnp.concatenate(split(block_map), axis=1), jnp.concatenate([s_hi, s_hi], axis=0)
                )
                states[h] = jnp.concatenate([grown[:, :width] + block_add, grown[:, width:]], axis=1)
        for h in range(HEADS_STEP):
            add_ref[s * HEADS_STEP + h] = states[h][:, :width]
            map_ref[s * HEADS_STEP + h] = states[h][:, width:]
            state_out[s * HEADS_STEP + h] = states[h][:, :width].astype(bf16)

        @pl.when(s == 0)
        def _():
            expected = jnp.where(first, 0, 1) + jnp.where(last, 0, 1) + head_count - 1
            pl.semaphore_wait(pltpu.get_barrier_semaphore(), expected)

        @pl.when(first & (seq_here < seq_count - 1))
        def _():
            for h in range(HEADS_STEP):
                hop(s * HEADS_STEP + h).start()

        @pl.when((s > 0) & (seq_here == 1) & (seq_here < seq_count - 1))
        def _():
            for h in range(HEADS_STEP):
                forward((s - 1) * HEADS_STEP + h)

        return carry

    lax.fori_loop(0, steps, states_step, 0)

    @pl.when(first)
    def _():
        state_in[...] = jnp.zeros_like(state_in)

    if steps > 1:
        @pl.when((seq_here > 1) & (seq_here < seq_count - 1))
        def _():
            for h in range((steps - 1) * HEADS_STEP):
                forward(h)

    def reads_step(s, carry):
        load(s, 2).wait()
        geo = []
        for b in range(blocks):
            start, seg_row, before, _ = geometry(b)
            seg_tok = segment(start + lax.broadcasted_iota(jnp.int32, (BLOCK, 1), 0))
            geo.append(((tok_j // refl <= tok_i) & (seg_tok == seg_row), seg_tok == before))

        def read_weights(h, b):
            keys, row = near(s, b)
            qb, c_row = q_ref[s, toks(b), cols(h)], row(0, h)
            n_row = scale_ref[b, pl.ds(s * HEADS_STEP + h, 1), :]
            qf = qb.astype(f32)
            nq = lax.rsqrt(jnp.sum(qf * qf, axis=1, keepdims=True) + epsilon) * width ** (-0.5)
            ct = jnp.sum(jnp.where(pick_tok, c_row, 0.0), axis=1, keepdims=True)
            ratio = jnp.where(geo[b][0], jnp.exp(jnp.minimum(ct - c_row, 0.0)), 0.0)
            carried = (jnp.where(geo[b][1], jnp.exp(ct), 0.0) * nq) * qf
            return (ratio * mm_nt(qb, keys(h)) * nq * n_row).astype(bf16), carried

        weights = over(read_weights)

        def read(h, b, weight):
            got = mm(weight[0], wrote_ref[s * HEADS_STEP + h, b])
            return got[:, :width], (weight[1] - got[:, width:]).astype(bf16)

        for (h, b), (own, back) in zip(pairs, over(read, weights)):
            if b:
                moved = mm(back, prefix_ref[s * HEADS_STEP + h, b - 1])
                own, back = own + moved[:, :width], moved[:, width:].astype(bf16)
            oloc_ref[s * HEADS_STEP + h, toks(b), :] = own
            read_ref[s * HEADS_STEP + h, toks(b), :] = back
        return carry

    lax.fori_loop(0, steps, reads_step, 0)

    done = (steps - 1) * HEADS_STEP
    for g in range(0, heads, FINISH_GROUP):
        group = range(g, min(g + FINISH_GROUP, heads))

        for h in group:
            if h < done:
                @pl.when(last & (seq_here > 0))
                def _():
                    hop(h).wait_recv()
            else:
                @pl.when(last & (seq_here > 0))
                def _():
                    hop(h).wait_recv()

                @pl.when((seq_here > 0) & (seq_here < seq_count - 1))
                def _():
                    forward(h)

        for h in group:
            out = oloc_ref[h] + mm(read_ref[h], state_in[h])
            scale = lax.rsqrt(jnp.mean(out * out, axis=-1, keepdims=True) + epsilon)
            normed_ref[:, cols(h)] = (out * scale * gain_ref[...]).astype(bf16)

    load_weight.wait()
    piece = weight_ref.shape[1] // PIECES
    copies = []
    for slot, other in enumerate(others):
        rows = normed_ref[pl.ds(pl.multiple_of(other * chunk, chunk), chunk), :]
        for p in range(PIECES):
            part = pl.ds(p * piece, piece)
            part_out[slot, :, part] = mm(rows, weight_ref[:, part]).astype(bf16)
            copies.append(
                pltpu.make_async_remote_copy(
                    src_ref=part_out.at[slot, :, part],
                    dst_ref=part_in.at[slot, :, part],
                    send_sem=part_send.at[slot, p],
                    recv_sem=part_recv.at[slot, p],
                    device_id={"head": other},
                    device_id_type=MESH,
                )
            )
            copies[-1].start()
    rows = normed_ref[pl.ds(pl.multiple_of(head_here * chunk, chunk), chunk), :]
    for p in range(PIECES):
        part = pl.ds(p * piece, piece)
        own_ref[:, part] = mm(rows, weight_ref[:, part])
    for p in range(PIECES):
        part = pl.ds(p * piece, piece)
        total = own_ref[:, part].astype(bf16).astype(f32)
        for slot in range(len(others)):
            copies[slot * PIECES + p].wait_recv()
            total += part_in[slot, :, part].astype(f32)
        out_ref[:, part] = total.astype(bf16)
    for copy in copies:
        copy.wait_send()

    @pl.when(seq_here < seq_count - 1)
    def _():
        for h in range(heads):
            hop(h).wait_send()


def body(queries, reflect_keys, reflect_values, reflect_beta, log_decay, prompt_lengths, norm_gain, out_weight):
    tokens, refl, wide = reflect_keys.shape[1:]
    heads = log_decay.shape[2]
    width = wide // heads
    blocks = tokens // BLOCK
    sub = refl * BLOCK
    head_count = lax.axis_size("head")
    chunk, model = tokens // head_count, out_weight.shape[1]
    steps, slots = heads // HEADS_STEP, max(head_count - 1, 1)
    wide_step = HEADS_STEP * width
    beta, gate = reflect_beta[0].transpose(1, 2, 0), log_decay[0].T
    dma = pltpu.SemaphoreType.DMA
    anywhere, vmem = pl.BlockSpec(memory_space=pl.ANY), pl.BlockSpec(memory_space=pltpu.VMEM)
    out = pl.pallas_call(
        functools.partial(mixer_kernel, refl, blocks),
        in_specs=[
            pl.BlockSpec(memory_space=pltpu.SMEM),
            anywhere, anywhere, anywhere, anywhere, anywhere, vmem, anywhere,
        ],
        out_specs=vmem,
        out_shape=pltpu.VMEM((chunk, model), bf16),
        scratch_shapes=[
            pltpu.VMEM((steps, tokens, wide_step), bf16),
            pltpu.VMEM((steps, tokens, refl, wide_step), bf16),
            pltpu.VMEM((steps, tokens, refl, wide_step), bf16),
            pltpu.VMEM(beta.shape, f32),
            pltpu.VMEM(gate.shape, f32),
            dma((steps, 3)),
            pltpu.VMEM((blocks, 2, heads, sub), f32),
            pltpu.VMEM((blocks, heads, sub), f32),
            pltpu.VMEM((steps, tokens * refl, wide_step), bf16),
            pltpu.VMEM((heads, blocks, sub, 2 * width), bf16),
            pltpu.VMEM((heads, max(blocks - 1, 1), width, 2 * width), bf16),
            pltpu.VMEM((heads, tokens, width), f32),
            pltpu.VMEM((heads, tokens, width), bf16),
            pltpu.VMEM((heads, width, width), f32),
            pltpu.VMEM((heads, width, width), f32),
            pltpu.VMEM(out_weight.shape, bf16),
            dma((3,)),
            pltpu.VMEM((heads, width, width), bf16),
            pltpu.VMEM((heads, width, width), bf16),
            pltpu.VMEM((tokens, wide), bf16),
            pltpu.VMEM((chunk, model), f32),
            pltpu.VMEM((slots, chunk, model), bf16),
            pltpu.VMEM((slots, chunk, model), bf16),
            dma((heads,)), dma((heads,)), dma((slots, PIECES)), dma((slots, PIECES)),
        ],
        compiler_params=pltpu.CompilerParams(
            collective_id=0, has_side_effects=True, vmem_limit_bytes=56 * 2**20
        ),
    )(
        prompt_lengths,
        queries[0],
        reflect_keys[0],
        reflect_values[0],
        beta,
        gate,
        norm_gain[None],
        out_weight,
    )
    return out[None]


def solution(mesh):
    in_specs = (
        P(("parts", "rep"), "seq", "head"),
        P(("parts", "rep"), "seq", None, "head"),
        P(("parts", "rep"), "seq", None, "head"),
        P(("parts", "rep"), "seq", None, "head"),
        P(("parts", "rep"), "seq", "head"),
        P(("parts", "rep"), None),
        P(),
        P("head", None),
    )
    out_specs = P(("parts", "rep"), ("seq", "head"), None)
    return jax.shard_map(body, mesh=mesh, in_specs=in_specs, out_specs=out_specs, check_vma=False)
```

time: 40.4 us -> 36.6 us (0.906)
  Pallas kernels: 38.4 us -> 35.6 us
  local copies, waits for them, and re-layouts: 1.88 us -> 0.8 us
    pallas_call x1, Pallas kernels: 38.4 us -> 35.6 us  [body(): pl.pallas_call(functools.partial(mixer_kernel, refl, blocks), in_specs=[p...]
    unnamed x1, local copies, waits for them, and re-layouts: 1.88 us -> 0.8 us
where the time goes in v1:
time: 36.6 us; the launch traced here: 36.4 us
  Pallas kernels  35.6 us (97%)
  local copies, waits for them, and re-layouts  0.8 us (2%)
    pallas_call x1, Pallas kernels, body(): pl.pallas_call(functools.partial(mixer_kernel, refl, blocks), in_specs=[p...  35.6 us
    unnamed x1, local copies, waits for them, and re-layouts  0.8 us

profile of v1, /device:TPU:28, one launch (start us, length us, event | category | flops | bytes accessed | tf_op | source)
XLA Modules:
  0.0 36.4 jit_solution(440891099984088318)
XLA Ops:
  0.0 35.6 %shard_map.82 = bf16[128,2048]{1,0:T(8,128)(2,1)S(1)} custom-call(s32[1,6]{1,0:T(1,128)} %len_ref.1, bf16[256,1024]{1,0:T(8,128)(2,1)} %bitcast.14, bf16[256,2,1024]{2,1,0:T(2,128)(2,1)} %bitcast.12, bf16[256,2,1024]{2,1,0:T(2,128)(2,1)} %bitcast.13, f32[2,8,256]{2,1,0:T(8,128)} %bitcast.15, f32[8,256]{1,0:T(8,128)} %bitcast.16, f32[1,128]{1,0:T(1,128)} %bitcast.17, ...), custom_call_target="tpu_custom_call" | custom-call | tf_op jit(solution)/shard_map/pallas_call | solution.py:429
  35.6 0.8 %copy.10 = bf16[1,128,2048]{2,1,0:T(8,128)(2,1)} copy(bf16[1,128,2048]{2,1,0:T(8,128)(2,1)S(1)} %bitcast.11) | data formatting | bytes 1048576

commit v2 on v1

--- a/solution.py
+++ b/solution.py
@@ -11,6 +11,9 @@
 HEADS_STEP = 4
 FINISH_GROUP = 2
 PIECES = 4
+SHARE = 50
+SHARE_PARTS = 8
+MID_RELAYS = (1, 3)
 MESH = pl.DeviceIdType.MESH
 
 epsilon = 1e-06
@@ -53,12 +56,17 @@
     return got[:rows] + got[rows : 2 * rows] + got[2 * rows :]
 
 
+def sharing():
+    return all(lax.axis_size(name) == 2 for name in ("head", "parts", "rep"))
+
+
 def mixer_kernel(
     refl, blocks, len_ref, q_hbm, k_hbm, v_hbm, beta_hbm, gate_hbm, gain_ref, weight_hbm, out_ref,
     q_ref, k_ref, v_ref, beta_ref, gate_ref, in_sem,
     rows_ref, scale_ref, kflat_ref, wrote_ref, prefix_ref, oloc_ref, read_ref, add_ref, map_ref,
     weight_ref, weight_sem, state_in, state_out, normed_ref, own_ref, part_out, part_in,
     state_send, state_recv, part_send, part_recv,
+    peer_ref, rows_in, x_send, x_recv, y_send, y_recv, core_send, core_recv, norm_send, norm_recv,
 ):
     heads, width = add_ref.shape[:2]
     steps = heads // HEADS_STEP
@@ -70,6 +78,53 @@
     chunk = out_ref.shape[0]
     first, last = seq_here == 0, seq_here == seq_count - 1
     others = [lax.rem(head_here + d, head_count) for d in range(1, head_count)]
+    shared = peer_ref.shape[1] if sharing() else 0
+    parts_here, rep_here = lax.axis_index("parts"), lax.axis_index("rep")
+    quarter = peer_ref.shape[0] // 4
+    slab = quarter // SHARE_PARTS
+
+    def slab_rows(rep, parts, j, count=1):
+        at = (rep * 2 + parts) * quarter + j * slab
+        return pl.ds(pl.multiple_of(at, slab), count * slab)
+
+    def remote(src, dst, send, recv, device):
+        return pltpu.make_async_remote_copy(
+            src_ref=src, dst_ref=dst, send_sem=send, recv_sem=recv, device_id=device, device_id_type=MESH
+        )
+
+    def from_head(j):
+        rows = slab_rows(rep_here, parts_here, j)
+        return remote(
+            weight_hbm.at[rows, pl.ds(0, shared)], peer_ref.at[rows],
+            x_send.at[j], x_recv.at[j], {"head": 1 - head_here},
+        )
+
+    def over_parts(j, parts):
+        rows = slab_rows(rep_here, parts, j)
+        return remote(
+            peer_ref.at[rows], peer_ref.at[rows], y_send.at[j], y_recv.at[j], {"parts": 1 - parts_here}
+        )
+
+    def over_cores(j, rep):
+        count = 1 if j < SHARE_PARTS else SHARE_PARTS
+        parts, at = (parts_here, j) if j < SHARE_PARTS else (1 - parts_here, 0)
+        rows = slab_rows(rep, parts, at, count)
+        return remote(
+            peer_ref.at[rows], peer_ref.at[rows], core_send.at[j], core_recv.at[j], {"rep": 1 - rep_here}
+        )
+
+    def relay(j):
+        from_head(j).wait_recv()
+        over_parts(j, parts_here).start()
+        over_cores(j, rep_here).start()
+
+    def send_normed(h):
+        span = cols(h)
+        rows = pl.ds(pl.multiple_of(others[0] * chunk, chunk), chunk)
+        return remote(
+            normed_ref.at[rows, span], rows_in.at[:, span],
+            norm_send.at[h], norm_recv.at[h], {"head": 1 - head_here},
+        )
 
     def load(s, kind):
         span = pl.ds(pl.multiple_of(s * wide, wide), wide)
@@ -102,6 +157,9 @@
 
     for other in others:
         pl.semaphore_signal(barrier, inc=1, device_id={"head": other}, device_id_type=MESH)
+    if shared:
+        pl.semaphore_signal(barrier, inc=1, device_id={"parts": 1 - parts_here}, device_id_type=MESH)
+        pl.semaphore_signal(barrier, inc=1, device_id={"rep": 1 - rep_here}, device_id_type=MESH)
 
     offset = seq_here * tokens
     ends = []
@@ -129,6 +187,12 @@
         big = min(4 * size, sub)
         levels.append((row_i // big == col_i // big) & (row_i // size > col_i // size))
         size = big
+
+    expected = jnp.where(first, 0, 1) + jnp.where(last, 0, 1) + head_count - 1 + (2 if shared else 0)
+    pl.semaphore_wait(barrier, expected)
+    if shared:
+        for j in range(SHARE_PARTS):
+            from_head(j).start()
 
     load_gate.wait()
     load_beta.wait()
@@ -233,6 +297,12 @@
                 half + mm(pair[:, :sub].astype(bf16), half.astype(bf16))
                 for half, pair in zip(halves, both)
             ]
+
+        if shared:
+            @pl.when(s > 0)
+            def _():
+                for j in range(*MID_RELAYS):
+                    relay(j)
 
         def residual(h, b, inv, low):
             inv_b = inv.astype(bf16)
@@ -287,11 +357,6 @@
             map_ref[s * HEADS_STEP + h] = states[h][:, width:]
             state_out[s * HEADS_STEP + h] = states[h][:, :width].astype(bf16)
 
-        @pl.when(s == 0)
-        def _():
-            expected = jnp.where(first, 0, 1) + jnp.where(last, 0, 1) + head_count - 1
-            pl.semaphore_wait(pltpu.get_barrier_semaphore(), expected)
-
         @pl.when(first & (seq_here < seq_count - 1))
         def _():
             for h in range(HEADS_STEP):
@@ -302,9 +367,19 @@
             for h in range(HEADS_STEP):
                 forward((s - 1) * HEADS_STEP + h)
 
+        if shared:
+            @pl.when(s == 0)
+            def _():
+                for j in range(MID_RELAYS[0]):
+                    relay(j)
+
         return carry
 
     lax.fori_loop(0, steps, states_step, 0)
+    relayed = MID_RELAYS[1] if steps > 1 else MID_RELAYS[0]
+    if shared:
+        relay(relayed)
+        relayed += 1
 
     @pl.when(first)
     def _():
@@ -347,9 +422,14 @@
                 own, back = own + moved[:, :width], moved[:, width:].astype(bf16)
             oloc_ref[s * HEADS_STEP + h, toks(b), :] = own
             read_ref[s * HEADS_STEP + h, toks(b), :] = back
+        if shared:
+            @pl.when(s == 0)
+            def _():
+                relay(relayed)
         return carry
 
     lax.fori_loop(0, steps, reads_step, 0)
+    relayed += 1
 
     done = (steps - 1) * HEADS_STEP
     for g in range(0, heads, FINISH_GROUP):
@@ -374,14 +454,24 @@
             scale = lax.rsqrt(jnp.mean(out * out, axis=-1, keepdims=True) + epsilon)
             normed_ref[:, cols(h)] = (out * scale * gain_ref[...]).astype(bf16)
 
+        if shared:
+            for h in group:
+                send_normed(h).start()
+            if relayed < SHARE_PARTS:
+                relay(relayed)
+                relayed += 1
+
     load_weight.wait()
-    piece = weight_ref.shape[1] // PIECES
+    if shared:
+        for j in range(relayed, SHARE_PARTS):
+            relay(j)
+    piece = (weight_ref.shape[1] - shared) // PIECES
     copies = []
     for slot, other in enumerate(others):
         rows = normed_ref[pl.ds(pl.multiple_of(other * chunk, chunk), chunk), :]
         for p in range(PIECES):
             part = pl.ds(p * piece, piece)
-            part_out[slot, :, part] = mm(rows, weight_ref[:, part]).astype(bf16)
+            part_out[slot, :, part] = mm(rows, weight_ref[:, pl.ds(shared + p * piece, piece)]).astype(bf16)
             copies.append(
                 pltpu.make_async_remote_copy(
                     src_ref=part_out.at[slot, :, part],
@@ -394,18 +484,45 @@
             )
             copies[-1].start()
     rows = normed_ref[pl.ds(pl.multiple_of(head_here * chunk, chunk), chunk), :]
+    if shared:
+        for j in range(SHARE_PARTS):
+            over_parts(j, 1 - parts_here).wait_recv()
+        over_cores(SHARE_PARTS, rep_here).start()
+    for p in range(PIECES):
+        part = pl.ds(shared + p * piece, piece)
+        own_ref[:, part] = mm(rows, weight_ref[:, part])
+    if shared:
+        portion = shared // PIECES
+        for p in range(PIECES):
+            part = pl.ds(p * portion, portion)
+            own_ref[:, part] = mm(rows, weight_ref[:, part])
+        for j in range(SHARE_PARTS + 1):
+            over_cores(j, 1 - rep_here).wait_recv()
+        for h in range(heads):
+            send_normed(h).wait_recv()
+        for p in range(PIECES):
+            part = pl.ds(p * portion, portion)
+            peer = mm(rows_in[...], peer_ref[:, part])
+            total = own_ref[:, part].astype(bf16).astype(f32) + peer.astype(bf16).astype(f32)
+            out_ref[:, part] = total.astype(bf16)
     for p in range(PIECES):
         part = pl.ds(p * piece, piece)
-        own_ref[:, part] = mm(rows, weight_ref[:, part])
-    for p in range(PIECES):
-        part = pl.ds(p * piece, piece)
-        total = own_ref[:, part].astype(bf16).astype(f32)
+        spot = pl.ds(shared + p * piece, piece)
+        total = own_ref[:, spot].astype(bf16).astype(f32)
         for slot in range(len(others)):
             copies[slot * PIECES + p].wait_recv()
             total += part_in[slot, :, part].astype(f32)
-        out_ref[:, part] = total.astype(bf16)
+        out_ref[:, spot] = total.astype(bf16)
     for copy in copies:
         copy.wait_send()
+    if shared:
+        for j in range(SHARE_PARTS):
+            from_head(j).wait_send()
+            over_parts(j, parts_here).wait_send()
+        for j in range(SHARE_PARTS + 1):
+            over_cores(j, rep_here).wait_send()
+        for h in range(heads):
+            send_normed(h).wait_send()
 
     @pl.when(seq_here < seq_count - 1)
     def _():
@@ -423,6 +540,9 @@
     chunk, model = tokens // head_count, out_weight.shape[1]
     steps, slots = heads // HEADS_STEP, max(head_count - 1, 1)
     wide_step = HEADS_STEP * width
+    shared = model * SHARE // 128 // 100 * 128 if sharing() else 0
+    peer_shape = (out_weight.shape[0], shared) if shared else (32, 128)
+    rest = model - shared
     beta, gate = reflect_beta[0].transpose(1, 2, 0), log_decay[0].T
     dma = pltpu.SemaphoreType.DMA
     anywhere, vmem = pl.BlockSpec(memory_space=pl.ANY), pl.BlockSpec(memory_space=pltpu.VMEM)
@@ -456,9 +576,13 @@
             pltpu.VMEM((heads, width, width), bf16),
             pltpu.VMEM((tokens, wide), bf16),
             pltpu.VMEM((chunk, model), f32),
-            pltpu.VMEM((slots, chunk, model), bf16),
-            pltpu.VMEM((slots, chunk, model), bf16),
+            pltpu.VMEM((slots, chunk, rest), bf16),
+            pltpu.VMEM((slots, chunk, rest), bf16),
             dma((heads,)), dma((heads,)), dma((slots, PIECES)), dma((slots, PIECES)),
+            pltpu.VMEM(peer_shape, bf16),
+            pltpu.VMEM((chunk, wide), bf16),
+            dma((SHARE_PARTS,)), dma((SHARE_PARTS,)), dma((SHARE_PARTS,)), dma((SHARE_PARTS,)),
+            dma((SHARE_PARTS + 1,)), dma((SHARE_PARTS + 1,)), dma((heads,)), dma((heads,)),
         ],
         compiler_params=pltpu.CompilerParams(
             collective_id=0, has_side_effects=True, vmem_limit_bytes=56 * 2**20

time: 36.6 us -> 34.6 us (0.945)
  the two profiles are of different devices: /device:TPU:28 before, /device:TPU:16 now
where the time goes in v2:
time: 34.6 us; the launch traced here: 34.3 us
  Pallas kernels  33.5 us (97%)
  local copies, waits for them, and re-layouts  0.8 us (2%)
    pallas_call x1, Pallas kernels, body(): pl.pallas_call(functools.partial(mixer_kernel, refl, blocks), in_specs=[p...  33.5 us
    unnamed x1, local copies, waits for them, and re-layouts  0.8 us

profile of v2, /device:TPU:16, one launch (start us, length us, event | category | flops | bytes accessed | tf_op | source)
XLA Modules:
  0.0 34.3 jit_solution(16233260677410862233)
XLA Ops:
  0.0 33.5 %shard_map.82 = bf16[128,2048]{1,0:T(8,128)(2,1)S(1)} custom-call(s32[1,6]{1,0:T(1,128)} %len_ref.1, bf16[256,1024]{1,0:T(8,128)(2,1)} %bitcast.14, bf16[256,2,1024]{2,1,0:T(2,128)(2,1)} %bitcast.12, bf16[256,2,1024]{2,1,0:T(2,128)(2,1)} %bitcast.13, f32[2,8,256]{2,1,0:T(8,128)} %bitcast.15, f32[8,256]{1,0:T(8,128)} %bitcast.16, f32[1,128]{1,0:T(1,128)} %bitcast.17, ...), custom_call_target="tpu_custom_call" | custom-call | tf_op jit(solution)/shard_map/pallas_call | solution.py:549
  33.6 0.8 %copy.10 = bf16[1,128,2048]{2,1,0:T(8,128)(2,1)} copy(bf16[1,128,2048]{2,1,0:T(8,128)(2,1)S(1)} %bitcast.11) | data formatting | bytes 1048576

commit v3 on v2

--- a/solution.py
+++ b/solution.py
@@ -13,7 +13,8 @@
 PIECES = 4
 SHARE = 50
 SHARE_PARTS = 8
-MID_RELAYS = (1, 3)
+MID_RELAYS = (2, 4)
+TEAM = 2
 MESH = pl.DeviceIdType.MESH
 
 epsilon = 1e-06
@@ -64,8 +65,8 @@
     refl, blocks, len_ref, q_hbm, k_hbm, v_hbm, beta_hbm, gate_hbm, gain_ref, weight_hbm, out_ref,
     q_ref, k_ref, v_ref, beta_ref, gate_ref, in_sem,
     rows_ref, scale_ref, kflat_ref, wrote_ref, prefix_ref, oloc_ref, read_ref, add_ref, map_ref,
-    weight_ref, weight_sem, state_in, state_out, normed_ref, own_ref, part_out, part_in,
-    state_send, state_recv, part_send, part_recv,
+    weight_ref, weight_sem, state_in, own_out, full_out, own_in, full_in, normed_ref, own_ref, part_out, part_in,
+    own_send, own_recv, full_send, full_recv, part_send, part_recv,
     peer_ref, rows_in, x_send, x_recv, y_send, y_recv, core_send, core_recv, norm_send, norm_recv,
 ):
     heads, width = add_ref.shape[:2]
@@ -147,13 +148,9 @@
 
     barrier = pltpu.get_barrier_semaphore()
 
-    @pl.when(seq_here > 0)
-    def _():
-        pl.semaphore_signal(barrier, inc=1, device_id={"seq": seq_here - 1}, device_id_type=MESH)
-
-    @pl.when(seq_here < seq_count - 1)
-    def _():
-        pl.semaphore_signal(barrier, inc=1, device_id={"seq": seq_here + 1}, device_id_type=MESH)
+    for move in (1, seq_count - 1):
+        other = lax.rem(seq_here + move, seq_count)
+        pl.semaphore_signal(barrier, inc=1, device_id={"seq": other}, device_id_type=MESH)
 
     for other in others:
         pl.semaphore_signal(barrier, inc=1, device_id={"head": other}, device_id_type=MESH)
@@ -188,8 +185,7 @@
         levels.append((row_i // big == col_i // big) & (row_i // size > col_i // size))
         size = big
 
-    expected = jnp.where(first, 0, 1) + jnp.where(last, 0, 1) + head_count - 1 + (2 if shared else 0)
-    pl.semaphore_wait(barrier, expected)
+    pl.semaphore_wait(barrier, 2 + head_count - 1 + (2 if shared else 0))
     if shared:
         for j in range(SHARE_PARTS):
             from_head(j).start()
@@ -229,23 +225,37 @@
     def column(values):
         return jnp.sum(jnp.where(eye, values, 0.0), axis=1, keepdims=True)
 
-    def hop(h):
-        return pltpu.make_async_remote_copy(
-            src_ref=state_out.at[h],
-            dst_ref=state_in.at[h],
-            send_sem=state_send.at[h],
-            recv_sem=state_recv.at[h],
-            device_id={"seq": lax.rem(seq_here + 1, seq_count)},
-            device_id_type=MESH,
-        )
-
-    def forward(h):
-        hop(h).wait_recv()
-        state = state_in[h]
+    reach = (seq_count * tokens // 2 - 2) // tokens
+    direct = reach <= 1
+    inner = (seq_here > 0) & (seq_here < seq_count - 1)
+    following = {"seq": lax.rem(seq_here + 1, seq_count)}
+
+    def send_own(h):
+        return remote(own_out.at[h], own_in.at[h], own_send.at[h], own_recv.at[h], following)
+
+    def send_full(h):
+        return remote(full_out.at[h], full_in.at[h], full_send.at[h], full_recv.at[h], following)
+
+    def pass_on(h, state):
         both = jnp.concatenate(split(map_ref[h]), axis=1)
         grown = add_ref[h] + mm(both, jnp.concatenate([state, state], axis=0))
-        state_out[h] = grown.astype(bf16)
-        hop(h).start()
+        full_out[h] = grown.astype(bf16)
+        send_full(h).start()
+
+    def forward(h):
+        if direct:
+            send_own(h).wait_recv()
+            pass_on(h, own_in[h])
+        else:
+            @pl.when(seq_here == 1)
+            def _():
+                send_own(h).wait_recv()
+                pass_on(h, own_in[h])
+
+            @pl.when(seq_here > 1)
+            def _():
+                send_full(h).wait_recv()
+                pass_on(h, full_in[h])
 
     def near(s, b):
         def keys(h):
@@ -304,18 +314,19 @@
                 for j in range(*MID_RELAYS):
                     relay(j)
 
+        @pl.when((s > 0) & inner & (direct | (seq_here == 1)))
+        def _():
+            for h in range(HEADS_STEP):
+                forward((s - 1) * HEADS_STEP + h)
+
         def residual(h, b, inv, low):
             inv_b = inv.astype(bf16)
             low_2 = jnp.concatenate(split(low), axis=1)
             return eye_f - inv_b.astype(f32) - mm(low_2, jnp.concatenate([inv_b, inv_b], axis=0))
 
-        resids = over(residual, invs, lows)
-
         def refine(h, b, inv, resid):
             inv_b = inv.astype(bf16)
             return inv_b.astype(f32) + mm(inv_b, resid.astype(bf16))
-
-        invs = over(refine, invs, resids)
 
         def write(h, b, inv, n_row):
             carry_row = jnp.where(geo[b][1], jnp.exp(row(0, h, b)), 0.0)
@@ -328,8 +339,6 @@
                 axis=1,
             )
 
-        writes = over(write, invs, n_rows)
-
         def block_step(h, b, wrote, n_col, c_col):
             wrote_ref[s * HEADS_STEP + h, b] = wrote.astype(bf16)
             c_end = row(0, h, b)[:, sub - 1 : sub]
@@ -341,31 +350,54 @@
             carry_end = jnp.where(geo[b][3], jnp.exp(c_end), 0.0)
             return moved[:, :width], carry_end * eye_f - moved[:, width:]
 
-        made = over(block_step, writes, n_cols, c_cols)
-        states = [jnp.concatenate(made[h * blocks], axis=1) for h in range(HEADS_STEP)]
-        for b in range(1, blocks):
-            for h in range(HEADS_STEP):
-                block_add, block_map = made[h * blocks + b]
+        made, states = {}, {}
+
+        def some(heads_now, stage, *lists):
+            return {(h, b): stage(h, b, *[l[h, b] for l in lists]) for h in heads_now for b in range(blocks)}
+
+        def scan(heads_now, b):
+            for h in heads_now:
+                if b == 0:
+                    states[h] = jnp.concatenate(made[h, 0], axis=1)
+                    continue
+                block_add, block_map = made[h, b]
                 s_hi = states[h].astype(bf16)
                 prefix_ref[s * HEADS_STEP + h, b - 1] = s_hi
                 grown = mm(
                     jnp.concatenate(split(block_map), axis=1), jnp.concatenate([s_hi, s_hi], axis=0)
                 )
                 states[h] = jnp.concatenate([grown[:, :width] + block_add, grown[:, width:]], axis=1)
-        for h in range(HEADS_STEP):
-            add_ref[s * HEADS_STEP + h] = states[h][:, :width]
-            map_ref[s * HEADS_STEP + h] = states[h][:, width:]
-            state_out[s * HEADS_STEP + h] = states[h][:, :width].astype(bf16)
-
-        @pl.when(first & (seq_here < seq_count - 1))
-        def _():
-            for h in range(HEADS_STEP):
-                hop(s * HEADS_STEP + h).start()
-
-        @pl.when((s > 0) & (seq_here == 1) & (seq_here < seq_count - 1))
-        def _():
-            for h in range(HEADS_STEP):
-                forward((s - 1) * HEADS_STEP + h)
+
+        def finish(heads_now):
+            for h in heads_now:
+                at = s * HEADS_STEP + h
+                own_out[at] = states[h][:, :width].astype(bf16)
+                send_own(at).start()
+                add_ref[at] = states[h][:, :width]
+                map_ref[at] = states[h][:, width:]
+
+        named = lambda values: dict(zip(pairs, values))
+        lows, invs, n_rows, n_cols, c_cols = map(named, (lows, invs, n_rows, n_cols, c_cols))
+        teams = [list(range(h, min(h + TEAM, HEADS_STEP))) for h in range(0, HEADS_STEP, TEAM)]
+        pending = []
+
+        def catch_up(count):
+            for _ in range(count):
+                if pending:
+                    pending.pop(0)()
+
+        for team in teams:
+            resids = some(team, residual, invs, lows)
+            catch_up(2)
+            better = some(team, refine, invs, resids)
+            catch_up(1)
+            writes = some(team, write, better, n_rows)
+            catch_up(1)
+            made.update(some(team, block_step, writes, n_cols, c_cols))
+            catch_up(len(pending))
+            pending = [functools.partial(scan, team, b) for b in range(blocks)]
+            pending.append(functools.partial(finish, team))
+        catch_up(len(pending))
 
         if shared:
             @pl.when(s == 0)
@@ -378,17 +410,19 @@
     lax.fori_loop(0, steps, states_step, 0)
     relayed = MID_RELAYS[1] if steps > 1 else MID_RELAYS[0]
     if shared:
-        relay(relayed)
-        relayed += 1
+        for _ in range(2):
+            relay(relayed)
+            relayed += 1
 
     @pl.when(first)
     def _():
         state_in[...] = jnp.zeros_like(state_in)
 
-    if steps > 1:
-        @pl.when((seq_here > 1) & (seq_here < seq_count - 1))
+    done = (steps - 1) * HEADS_STEP
+    if done and not direct:
+        @pl.when(inner & (seq_here > 1))
         def _():
-            for h in range((steps - 1) * HEADS_STEP):
+            for h in range(done):
                 forward(h)
 
     def reads_step(s, carry):
@@ -431,23 +465,30 @@
     lax.fori_loop(0, steps, reads_step, 0)
     relayed += 1
 
-    done = (steps - 1) * HEADS_STEP
     for g in range(0, heads, FINISH_GROUP):
         group = range(g, min(g + FINISH_GROUP, heads))
 
         for h in group:
-            if h < done:
-                @pl.when(last & (seq_here > 0))
-                def _():
-                    hop(h).wait_recv()
-            else:
-                @pl.when(last & (seq_here > 0))
-                def _():
-                    hop(h).wait_recv()
-
-                @pl.when((seq_here > 0) & (seq_here < seq_count - 1))
+            if h >= done:
+                @pl.when(inner)
                 def _():
                     forward(h)
+
+            @pl.when(last & (seq_here == 1))
+            def _():
+                send_own(h).wait_recv()
+
+            @pl.when((seq_here > 1) & (direct | last))
+            def _():
+                send_full(h).wait_recv()
+
+            @pl.when(seq_here == 1)
+            def _():
+                state_in[h] = own_in[h]
+
+            @pl.when(seq_here > 1)
+            def _():
+                state_in[h] = full_in[h]
 
         for h in group:
             out = oloc_ref[h] + mm(read_ref[h], state_in[h])
@@ -524,10 +565,18 @@
         for h in range(heads):
             send_normed(h).wait_send()
 
-    @pl.when(seq_here < seq_count - 1)
+    @pl.when(first | ((seq_here > 1) & (last | (not direct))))
     def _():
         for h in range(heads):
-            hop(h).wait_send()
+            send_own(h).wait_recv()
+
+    for h in range(heads):
+        send_own(h).wait_send()
+
+    @pl.when(inner)
+    def _():
+        for h in range(heads):
+            send_full(h).wait_send()
 
 
 def body(queries, reflect_keys, reflect_values, reflect_beta, log_decay, prompt_lengths, norm_gain, out_weight):
@@ -572,13 +621,12 @@
             pltpu.VMEM((heads, width, width), f32),
             pltpu.VMEM(out_weight.shape, bf16),
             dma((3,)),
-            pltpu.VMEM((heads, width, width), bf16),
-            pltpu.VMEM((heads, width, width), bf16),
+            *[pltpu.VMEM((heads, width, width), bf16)] * 5,
             pltpu.VMEM((tokens, wide), bf16),
             pltpu.VMEM((chunk, model), f32),
             pltpu.VMEM((slots, chunk, rest), bf16),
             pltpu.VMEM((slots, chunk, rest), bf16),
-            dma((heads,)), dma((heads,)), dma((slots, PIECES)), dma((slots, PIECES)),
+            *[dma((heads,))] * 4, dma((slots, PIECES)), dma((slots, PIECES)),
             pltpu.VMEM(peer_shape, bf16),
             pltpu.VMEM((chunk, wide), bf16),
             dma((SHARE_PARTS,)), dma((SHARE_PARTS,)), dma((SHARE_PARTS,)), dma((SHARE_PARTS,)),

time: 34.6 us -> 35 us (1.012)
  the two profiles are of different devices: /device:TPU:16 before, /device:TPU:0 now
where the time goes in v3:
time: 35 us; the launch traced here: 34.8 us
  Pallas kernels  34 us (97%)
  local copies, waits for them, and re-layouts  0.8 us (2%)
    pallas_call x1, Pallas kernels, body(): pl.pallas_call(functools.partial(mixer_kernel, refl, blocks), in_specs=[p...  34 us
    unnamed x1, local copies, waits for them, and re-layouts  0.8 us

profile of v3, /device:TPU:0, one launch (start us, length us, event | category | flops | bytes accessed | tf_op | source)
XLA Modules:
  0.0 34.8 jit_solution(5335480401069532634)
XLA Ops:
  0.0 34.0 %shard_map.82 = bf16[128,2048]{1,0:T(8,128)(2,1)S(1)} custom-call(s32[1,6]{1,0:T(1,128)} %len_ref.1, bf16[256,1024]{1,0:T(8,128)(2,1)} %bitcast.14, bf16[256,2,1024]{2,1,0:T(2,128)(2,1)} %bitcast.12, bf16[256,2,1024]{2,1,0:T(2,128)(2,1)} %bitcast.13, f32[2,8,256]{2,1,0:T(8,128)} %bitcast.15, f32[8,256]{1,0:T(8,128)} %bitcast.16, f32[1,128]{1,0:T(1,128)} %bitcast.17, ...), custom_call_target="tpu_custom_call" | custom-call | tf_op jit(solution)/shard_map/pallas_call | solution.py:598
  34.0 0.8 %copy.10 = bf16[1,128,2048]{2,1,0:T(8,128)(2,1)} copy(bf16[1,128,2048]{2,1,0:T(8,128)(2,1)S(1)} %bitcast.11) | data formatting | bytes 1048576

commit v4 on v3

--- a/solution.py
+++ b/solution.py
@@ -10,10 +10,10 @@
 BLOCK = 64
 HEADS_STEP = 4
 FINISH_GROUP = 2
-PIECES = 4
-SHARE = 50
+PIECE = 256
+SHARE = 63
 SHARE_PARTS = 8
-MID_RELAYS = (2, 4)
+RELAYS = (1, 3, 5, 6, 7)
 TEAM = 2
 MESH = pl.DeviceIdType.MESH
 
@@ -84,9 +84,8 @@
     quarter = peer_ref.shape[0] // 4
     slab = quarter // SHARE_PARTS
 
-    def slab_rows(rep, parts, j, count=1):
-        at = (rep * 2 + parts) * quarter + j * slab
-        return pl.ds(pl.multiple_of(at, slab), count * slab)
+    def slab_rows(rep, parts, j):
+        return pl.ds(pl.multiple_of((rep * 2 + parts) * quarter + j * slab, slab), slab)
 
     def remote(src, dst, send, recv, device):
         return pltpu.make_async_remote_copy(
@@ -107,9 +106,8 @@
         )
 
     def over_cores(j, rep):
-        count = 1 if j < SHARE_PARTS else SHARE_PARTS
-        parts, at = (parts_here, j) if j < SHARE_PARTS else (1 - parts_here, 0)
-        rows = slab_rows(rep, parts, at, count)
+        parts = parts_here if j < SHARE_PARTS else 1 - parts_here
+        rows = slab_rows(rep, parts, j % SHARE_PARTS)
         return remote(
             peer_ref.at[rows], peer_ref.at[rows], core_send.at[j], core_recv.at[j], {"rep": 1 - rep_here}
         )
@@ -148,9 +146,13 @@
 
     barrier = pltpu.get_barrier_semaphore()
 
-    for move in (1, seq_count - 1):
-        other = lax.rem(seq_here + move, seq_count)
-        pl.semaphore_signal(barrier, inc=1, device_id={"seq": other}, device_id_type=MESH)
+    @pl.when(seq_here > 0)
+    def _():
+        pl.semaphore_signal(barrier, inc=1, device_id={"seq": seq_here - 1}, device_id_type=MESH)
+
+    @pl.when(seq_here < seq_count - 1)
+    def _():
+        pl.semaphore_signal(barrier, inc=1, device_id={"seq": seq_here + 1}, device_id_type=MESH)
 
     for other in others:
         pl.semaphore_signal(barrier, inc=1, device_id={"head": other}, device_id_type=MESH)
@@ -185,7 +187,8 @@
         levels.append((row_i // big == col_i // big) & (row_i // size > col_i // size))
         size = big
 
-    pl.semaphore_wait(barrier, 2 + head_count - 1 + (2 if shared else 0))
+    expected = jnp.where(first, 0, 1) + jnp.where(last, 0, 1) + head_count - 1 + (2 if shared else 0)
+    pl.semaphore_wait(barrier, expected)
     if shared:
         for j in range(SHARE_PARTS):
             from_head(j).start()
@@ -229,9 +232,17 @@
     direct = reach <= 1
     inner = (seq_here > 0) & (seq_here < seq_count - 1)
     following = {"seq": lax.rem(seq_here + 1, seq_count)}
+    beside = {"seq": jnp.where(last, seq_count - 2, seq_here + 1)}
+    spare = jnp.where(last, heads, 0)
 
     def send_own(h):
+        return remote(own_out.at[h], own_in.at[h + spare], own_send.at[h], own_recv.at[h + spare], beside)
+
+    def take_own(h):
         return remote(own_out.at[h], own_in.at[h], own_send.at[h], own_recv.at[h], following)
+
+    def take_spare(h):
+        return remote(own_out.at[h], own_in.at[heads + h], own_send.at[h], own_recv.at[heads + h], following)
 
     def send_full(h):
         return remote(full_out.at[h], full_in.at[h], full_send.at[h], full_recv.at[h], following)
@@ -244,12 +255,12 @@
 
     def forward(h):
         if direct:
-            send_own(h).wait_recv()
+            take_own(h).wait_recv()
             pass_on(h, own_in[h])
         else:
             @pl.when(seq_here == 1)
             def _():
-                send_own(h).wait_recv()
+                take_own(h).wait_recv()
                 pass_on(h, own_in[h])
 
             @pl.when(seq_here > 1)
@@ -311,7 +322,7 @@
         if shared:
             @pl.when(s > 0)
             def _():
-                for j in range(*MID_RELAYS):
+                for j in range(RELAYS[0], RELAYS[1]):
                     relay(j)
 
         @pl.when((s > 0) & inner & (direct | (seq_here == 1)))
@@ -402,15 +413,15 @@
         if shared:
             @pl.when(s == 0)
             def _():
-                for j in range(MID_RELAYS[0]):
+                for j in range(RELAYS[0]):
                     relay(j)
 
         return carry
 
     lax.fori_loop(0, steps, states_step, 0)
-    relayed = MID_RELAYS[1] if steps > 1 else MID_RELAYS[0]
-    if shared:
-        for _ in range(2):
+    relayed = RELAYS[1] if steps > 1 else RELAYS[0]
+    if shared:
+        while relayed < RELAYS[2]:
             relay(relayed)
             relayed += 1
 
@@ -456,27 +467,35 @@
                 own, back = own + moved[:, :width], moved[:, width:].astype(bf16)
             oloc_ref[s * HEADS_STEP + h, toks(b), :] = own
             read_ref[s * HEADS_STEP + h, toks(b), :] = back
-        if shared:
-            @pl.when(s == 0)
-            def _():
+        return carry
+
+    lax.fori_loop(0, steps, reads_step, 0)
+    if shared:
+        while relayed < RELAYS[3]:
+            relay(relayed)
+            relayed += 1
+
+    @pl.when(inner)
+    def _():
+        for h in range(done, heads):
+            forward(h)
+
+    if shared:
+        while relayed < RELAYS[4]:
+            relay(relayed)
+            relayed += 1
+
+    for g in range(0, heads, FINISH_GROUP):
+        if shared and g >= done:
+            while relayed < SHARE_PARTS:
                 relay(relayed)
-        return carry
-
-    lax.fori_loop(0, steps, reads_step, 0)
-    relayed += 1
-
-    for g in range(0, heads, FINISH_GROUP):
+                relayed += 1
         group = range(g, min(g + FINISH_GROUP, heads))
 
         for h in group:
-            if h >= done:
-                @pl.when(inner)
-                def _():
-                    forward(h)
-
             @pl.when(last & (seq_here == 1))
             def _():
-                send_own(h).wait_recv()
+                take_own(h).wait_recv()
 
             @pl.when((seq_here > 1) & (direct | last))
             def _():
@@ -498,19 +517,13 @@
         if shared:
             for h in group:
                 send_normed(h).start()
-            if relayed < SHARE_PARTS:
-                relay(relayed)
-                relayed += 1
 
     load_weight.wait()
-    if shared:
-        for j in range(relayed, SHARE_PARTS):
-            relay(j)
-    piece = (weight_ref.shape[1] - shared) // PIECES
+    piece, pieces = PIECE, (weight_ref.shape[1] - shared) // PIECE
     copies = []
     for slot, other in enumerate(others):
         rows = normed_ref[pl.ds(pl.multiple_of(other * chunk, chunk), chunk), :]
-        for p in range(PIECES):
+        for p in range(pieces):
             part = pl.ds(p * piece, piece)
             part_out[slot, :, part] = mm(rows, weight_ref[:, pl.ds(shared + p * piece, piece)]).astype(bf16)
             copies.append(
@@ -528,30 +541,29 @@
     if shared:
         for j in range(SHARE_PARTS):
             over_parts(j, 1 - parts_here).wait_recv()
-        over_cores(SHARE_PARTS, rep_here).start()
-    for p in range(PIECES):
+            over_cores(SHARE_PARTS + j, rep_here).start()
+    for p in range(pieces):
         part = pl.ds(shared + p * piece, piece)
         own_ref[:, part] = mm(rows, weight_ref[:, part])
     if shared:
-        portion = shared // PIECES
-        for p in range(PIECES):
-            part = pl.ds(p * portion, portion)
+        for p in range(shared // piece):
+            part = pl.ds(p * piece, piece)
             own_ref[:, part] = mm(rows, weight_ref[:, part])
-        for j in range(SHARE_PARTS + 1):
+        for j in range(2 * SHARE_PARTS):
             over_cores(j, 1 - rep_here).wait_recv()
         for h in range(heads):
             send_normed(h).wait_recv()
-        for p in range(PIECES):
-            part = pl.ds(p * portion, portion)
+        for p in range(shared // piece):
+            part = pl.ds(p * piece, piece)
             peer = mm(rows_in[...], peer_ref[:, part])
             total = own_ref[:, part].astype(bf16).astype(f32) + peer.astype(bf16).astype(f32)
             out_ref[:, part] = total.astype(bf16)
-    for p in range(PIECES):
+    for p in range(pieces):
         part = pl.ds(p * piece, piece)
         spot = pl.ds(shared + p * piece, piece)
         total = own_ref[:, spot].astype(bf16).astype(f32)
         for slot in range(len(others)):
-            copies[slot * PIECES + p].wait_recv()
+            copies[slot * pieces + p].wait_recv()
             total += part_in[slot, :, part].astype(f32)
         out_ref[:, spot] = total.astype(bf16)
     for copy in copies:
@@ -560,15 +572,20 @@
         for j in range(SHARE_PARTS):
             from_head(j).wait_send()
             over_parts(j, parts_here).wait_send()
-        for j in range(SHARE_PARTS + 1):
+        for j in range(2 * SHARE_PARTS):
             over_cores(j, rep_here).wait_send()
         for h in range(heads):
             send_normed(h).wait_send()
 
-    @pl.when(first | ((seq_here > 1) & (last | (not direct))))
+    @pl.when((seq_here > 1) & (last | (not direct)))
     def _():
         for h in range(heads):
-            send_own(h).wait_recv()
+            take_own(h).wait_recv()
+
+    @pl.when(seq_here == seq_count - 2)
+    def _():
+        for h in range(heads):
+            take_spare(h).wait_recv()
 
     for h in range(heads):
         send_own(h).wait_send()
@@ -589,9 +606,10 @@
     chunk, model = tokens // head_count, out_weight.shape[1]
     steps, slots = heads // HEADS_STEP, max(head_count - 1, 1)
     wide_step = HEADS_STEP * width
-    shared = model * SHARE // 128 // 100 * 128 if sharing() else 0
+    shared = model * SHARE // PIECE // 100 * PIECE if sharing() else 0
     peer_shape = (out_weight.shape[0], shared) if shared else (32, 128)
     rest = model - shared
+    pieces = rest // PIECE
     beta, gate = reflect_beta[0].transpose(1, 2, 0), log_decay[0].T
     dma = pltpu.SemaphoreType.DMA
     anywhere, vmem = pl.BlockSpec(memory_space=pl.ANY), pl.BlockSpec(memory_space=pltpu.VMEM)
@@ -621,16 +639,18 @@
             pltpu.VMEM((heads, width, width), f32),
             pltpu.VMEM(out_weight.shape, bf16),
             dma((3,)),
-            *[pltpu.VMEM((heads, width, width), bf16)] * 5,
+            *[pltpu.VMEM((heads, width, width), bf16)] * 3,
+            pltpu.VMEM((2 * heads, width, width), bf16),
+            pltpu.VMEM((heads, width, width), bf16),
             pltpu.VMEM((tokens, wide), bf16),
             pltpu.VMEM((chunk, model), f32),
             pltpu.VMEM((slots, chunk, rest), bf16),
             pltpu.VMEM((slots, chunk, rest), bf16),
-            *[dma((heads,))] * 4, dma((slots, PIECES)), dma((slots, PIECES)),
+            dma((heads,)), dma((2 * heads,)), dma((heads,)), dma((heads,)), dma((slots, pieces)), dma((slots, pieces)),
             pltpu.VMEM(peer_shape, bf16),
             pltpu.VMEM((chunk, wide), bf16),
             dma((SHARE_PARTS,)), dma((SHARE_PARTS,)), dma((SHARE_PARTS,)), dma((SHARE_PARTS,)),
-            dma((SHARE_PARTS + 1,)), dma((SHARE_PARTS + 1,)), dma((heads,)), dma((heads,)),
+            dma((2 * SHARE_PARTS,)), dma((2 * SHARE_PARTS,)), dma((heads,)), dma((heads,)),
         ],
         compiler_params=pltpu.CompilerParams(
             collective_id=0, has_side_effects=True, vmem_limit_bytes=56 * 2**20

time: 35 us -> 32.5 us (0.929)
  the two profiles are of different devices: /device:TPU:0 before, /device:TPU:16 now
where the time goes in v4:
time: 32.5 us; the launch traced here: 32.4 us
  Pallas kernels  31.6 us (97%)
  local copies, waits for them, and re-layouts  0.8 us (2%)
    pallas_call x1, Pallas kernels, body(): pl.pallas_call(functools.partial(mixer_kernel, refl, blocks), in_specs=[p...  31.6 us
    unnamed x1, local copies, waits for them, and re-layouts  0.8 us

profile of v4, /device:TPU:16, one launch (start us, length us, event | category | flops | bytes accessed | tf_op | source)
XLA Modules:
  0.0 32.4 jit_solution(190802179976680888)
XLA Ops:
  0.0 31.6 %shard_map.82 = bf16[128,2048]{1,0:T(8,128)(2,1)S(1)} custom-call(s32[1,6]{1,0:T(1,128)} %len_ref.1, bf16[256,1024]{1,0:T(8,128)(2,1)} %bitcast.14, bf16[256,2,1024]{2,1,0:T(2,128)(2,1)} %bitcast.12, bf16[256,2,1024]{2,1,0:T(2,128)(2,1)} %bitcast.13, f32[2,8,256]{2,1,0:T(8,128)} %bitcast.15, f32[8,256]{1,0:T(8,128)} %bitcast.16, f32[1,128]{1,0:T(1,128)} %bitcast.17, ...), custom_call_target="tpu_custom_call" | custom-call | tf_op jit(solution)/shard_map/pallas_call | solution.py:616
  31.6 0.8 %copy.10 = bf16[1,128,2048]{2,1,0:T(8,128)(2,1)} copy(bf16[1,128,2048]{2,1,0:T(8,128)(2,1)S(1)} %bitcast.11) | data formatting | bytes 1048576

commit v5 on v4

--- a/solution.py
+++ b/solution.py
@@ -1,4 +1,5 @@
 import functools
+import math
 
 import jax
 import jax.numpy as jnp
@@ -62,8 +63,8 @@
 
 
 def mixer_kernel(
-    refl, blocks, len_ref, q_hbm, k_hbm, v_hbm, beta_hbm, gate_hbm, gain_ref, weight_hbm, out_ref,
-    q_ref, k_ref, v_ref, beta_ref, gate_ref, in_sem,
+    refl, blocks, len_hbm, q_hbm, k_hbm, v_hbm, beta_hbm, gate_hbm, gain_hbm, weight_hbm, out_ref,
+    len_ref, q_ref, k_ref, v_ref, beta_ref, gate_ref, gain_ref, in_sem, ready_sem,
     rows_ref, scale_ref, kflat_ref, wrote_ref, prefix_ref, oloc_ref, read_ref, add_ref, map_ref,
     weight_ref, weight_sem, state_in, own_out, full_out, own_in, full_in, normed_ref, own_ref, part_out, part_in,
     own_send, own_recv, full_send, full_recv, part_send, part_recv,
@@ -125,6 +126,18 @@
             norm_send.at[h], norm_recv.at[h], {"head": 1 - head_here},
         )
 
+    barrier = pltpu.get_barrier_semaphore()
+
+    @pl.when(seq_here < seq_count - 1)
+    def _():
+        pl.semaphore_signal(barrier, inc=1, device_id={"seq": seq_here + 1}, device_id_type=MESH)
+
+    for other in others:
+        pl.semaphore_signal(barrier, inc=1, device_id={"head": other}, device_id_type=MESH)
+    if shared:
+        pl.semaphore_signal(barrier, inc=1, device_id={"parts": 1 - parts_here}, device_id_type=MESH)
+        pl.semaphore_signal(barrier, inc=1, device_id={"rep": 1 - rep_here}, device_id_type=MESH)
+
     def load(s, kind):
         span = pl.ds(pl.multiple_of(s * wide, wide), wide)
         src, dst = [
@@ -135,6 +148,9 @@
     load_beta = pltpu.make_async_copy(beta_hbm, beta_ref, weight_sem.at[1])
     load_gate = pltpu.make_async_copy(gate_hbm, gate_ref, weight_sem.at[2])
     load_weight = pltpu.make_async_copy(weight_hbm, weight_ref, weight_sem.at[0])
+    load_len = pltpu.make_async_copy(len_hbm, len_ref, weight_sem.at[3])
+    load_gain = pltpu.make_async_copy(gain_hbm, gain_ref, weight_sem.at[4])
+    load_len.start()
     load_gate.start()
     load_beta.start()
     for s in range(steps):
@@ -142,23 +158,18 @@
         load(s, 1).start()
     for s in range(steps):
         load(s, 2).start()
+    load_gain.start()
     load_weight.start()
-
-    barrier = pltpu.get_barrier_semaphore()
+    pl.semaphore_wait(barrier, jnp.where(first, 0, 1) + head_count - 1 + (2 if shared else 0))
+    if shared:
+        for j in range(SHARE_PARTS):
+            from_head(j).start()
 
     @pl.when(seq_here > 0)
     def _():
-        pl.semaphore_signal(barrier, inc=1, device_id={"seq": seq_here - 1}, device_id_type=MESH)
-
-    @pl.when(seq_here < seq_count - 1)
-    def _():
-        pl.semaphore_signal(barrier, inc=1, device_id={"seq": seq_here + 1}, device_id_type=MESH)
-
-    for other in others:
-        pl.semaphore_signal(barrier, inc=1, device_id={"head": other}, device_id_type=MESH)
-    if shared:
-        pl.semaphore_signal(barrier, inc=1, device_id={"parts": 1 - parts_here}, device_id_type=MESH)
-        pl.semaphore_signal(barrier, inc=1, device_id={"rep": 1 - rep_here}, device_id_type=MESH)
+        pl.semaphore_signal(ready_sem, inc=1, device_id={"seq": seq_here - 1}, device_id_type=MESH)
+
+    load_len.wait()
 
     offset = seq_here * tokens
     ends = []
@@ -187,12 +198,6 @@
         levels.append((row_i // big == col_i // big) & (row_i // size > col_i // size))
         size = big
 
-    expected = jnp.where(first, 0, 1) + jnp.where(last, 0, 1) + head_count - 1 + (2 if shared else 0)
-    pl.semaphore_wait(barrier, expected)
-    if shared:
-        for j in range(SHARE_PARTS):
-            from_head(j).start()
-
     load_gate.wait()
     load_beta.wait()
     table = sub_rows(gate_ref[...], jnp.where(tok_i <= tok_j // refl, 1.0, 0.0).astype(bf16), blocks)
@@ -201,8 +206,9 @@
         pick = jnp.where(tok_i * refl + j == tok_j, 1.0, 0.0).astype(bf16)
         total += sub_rows(beta_ref[j], pick, blocks)
     for b in range(blocks):
-        rows_ref[b, 0] = table[:, b * sub : (b + 1) * sub]
+        rows_ref[b, 0] = table[:, b * sub : (b + 1) * sub] * math.log2(math.e)
         rows_ref[b, 1] = total[:, b * sub : (b + 1) * sub]
+        rows_ref[b, 2] = rows_ref[b, 0] + jnp.log2(rows_ref[b, 1])
 
     def geometry(b):
         start = offset + b * BLOCK
@@ -286,25 +292,21 @@
         for b in range(blocks):
             start, seg_row, before, last_seg = geometry(b)
             seg_col = segment(start + lax.broadcasted_iota(jnp.int32, (sub, 1), 0) // refl)
-            incl = (row_i >= col_i) & (seg_col == seg_row)
-            geo.append((incl, seg_row == before, seg_col == last_seg, last_seg == before))
+            incl = (row_i > col_i) & (seg_col == seg_row)
+            geo.append((incl, seg_row == before, seg_row == last_seg, last_seg == before))
 
         for h, b in pairs:
             kflat_ref[s, b * sub : (b + 1) * sub, cols(h)] = k_ref[s, toks(b), :, cols(h)].reshape(sub, width)
 
         def scales(h, b):
             gram = mm_nt(keys(h, b), keys(h, b))
-            diag = jnp.where(eye, gram, 0.0)
-            n_row = lax.rsqrt(jnp.sum(diag, axis=0, keepdims=True) + epsilon)
-            n_col = lax.rsqrt(jnp.sum(diag, axis=1, keepdims=True) + epsilon)
+            square = jnp.sum(jnp.where(eye, gram, 0.0), axis=0, keepdims=True) + epsilon
+            n_log, n_row = -0.5 * jnp.log2(square), lax.rsqrt(square)
             scale_ref[b, pl.ds(s * HEADS_STEP + h, 1), :] = n_row
-            c_row = row(0, h, b)
-            c_col = column(c_row)
-            ratio = jnp.where(geo[b][0], jnp.exp(jnp.minimum(c_col - c_row, 0.0)), 0.0)
-            low = jnp.where(eye, 0.0, (column(row(1, h, b)) * n_col) * ratio * gram * n_row)
-            return low, n_row, n_col, c_col
-
-        lows, n_rows, n_cols, c_cols = zip(*over(scales))
+            factor = jnp.exp2(column(row(2, h, b) + n_log) + (n_log - row(0, h, b)))
+            return jnp.where(geo[b][0], factor * gram, 0.0), n_row
+
+        lows, n_rows = zip(*over(scales))
         invs = [eye_f - jnp.where(row_i // refl == col_i // refl, low, 0.0) for low in lows]
         for mask in levels:
             heads_b = [inv.astype(bf16) for inv in invs]
@@ -325,6 +327,10 @@
                 for j in range(RELAYS[0], RELAYS[1]):
                     relay(j)
 
+        @pl.when((s == 0) & (seq_here < seq_count - 1))
+        def _():
+            pl.semaphore_wait(ready_sem, 1)
+
         @pl.when((s > 0) & inner & (direct | (seq_here == 1)))
         def _():
             for h in range(HEADS_STEP):
@@ -340,7 +346,7 @@
             return inv_b.astype(f32) + mm(inv_b, resid.astype(bf16))
 
         def write(h, b, inv, n_row):
-            carry_row = jnp.where(geo[b][1], jnp.exp(row(0, h, b)), 0.0)
+            carry_row = jnp.where(geo[b][1], jnp.exp2(row(0, h, b)), 0.0)
             by_beta = inv * row(1, h, b)
             tv = jnp.concatenate(split(by_beta), axis=1)
             tk = jnp.concatenate(split(by_beta * (carry_row * n_row)), axis=1)
@@ -350,15 +356,16 @@
                 axis=1,
             )
 
-        def block_step(h, b, wrote, n_col, c_col):
+        def block_step(h, b, wrote, n_row):
             wrote_ref[s * HEADS_STEP + h, b] = wrote.astype(bf16)
-            c_end = row(0, h, b)[:, sub - 1 : sub]
-            e_col = jnp.where(geo[b][2], jnp.exp(jnp.minimum(c_end - c_col, 0.0)), 0.0) * n_col
+            c_row = row(0, h, b)
+            c_end = c_row[:, sub - 1 : sub]
+            e_row = jnp.where(geo[b][2], jnp.exp2(jnp.minimum(c_end - c_row, 0.0)), 0.0) * n_row
             kb = keys(h, b)
             moved = mm_tn(
-                jnp.concatenate([kb, kb], axis=0), jnp.concatenate(split(wrote * e_col), axis=0)
+                jnp.concatenate([kb, kb], axis=0), jnp.concatenate(split(wrote * column(e_row)), axis=0)
             )
-            carry_end = jnp.where(geo[b][3], jnp.exp(c_end), 0.0)
+            carry_end = jnp.where(geo[b][3], jnp.exp2(c_end), 0.0)
             return moved[:, :width], carry_end * eye_f - moved[:, width:]
 
         made, states = {}, {}
@@ -388,7 +395,7 @@
                 map_ref[at] = states[h][:, width:]
 
         named = lambda values: dict(zip(pairs, values))
-        lows, invs, n_rows, n_cols, c_cols = map(named, (lows, invs, n_rows, n_cols, c_cols))
+        lows, invs, n_rows = map(named, (lows, invs, n_rows))
         teams = [list(range(h, min(h + TEAM, HEADS_STEP))) for h in range(0, HEADS_STEP, TEAM)]
         pending = []
 
@@ -404,7 +411,7 @@
             catch_up(1)
             writes = some(team, write, better, n_rows)
             catch_up(1)
-            made.update(some(team, block_step, writes, n_cols, c_cols))
+            made.update(some(team, block_step, writes, n_rows))
             catch_up(len(pending))
             pending = [functools.partial(scan, team, b) for b in range(blocks)]
             pending.append(functools.partial(finish, team))
@@ -451,8 +458,8 @@
             qf = qb.astype(f32)
             nq = lax.rsqrt(jnp.sum(qf * qf, axis=1, keepdims=True) + epsilon) * width ** (-0.5)
             ct = jnp.sum(jnp.where(pick_tok, c_row, 0.0), axis=1, keepdims=True)
-            ratio = jnp.where(geo[b][0], jnp.exp(jnp.minimum(ct - c_row, 0.0)), 0.0)
-            carried = (jnp.where(geo[b][1], jnp.exp(ct), 0.0) * nq) * qf
+            ratio = jnp.where(geo[b][0], jnp.exp2(jnp.minimum(ct - c_row, 0.0)), 0.0)
+            carried = (jnp.where(geo[b][1], jnp.exp2(ct), 0.0) * nq) * qf
             return (ratio * mm_nt(qb, keys(h)) * nq * n_row).astype(bf16), carried
 
         weights = over(read_weights)
@@ -485,6 +492,7 @@
             relay(relayed)
             relayed += 1
 
+    load_gain.wait()
     for g in range(0, heads, FINISH_GROUP):
         if shared and g >= done:
             while relayed < SHARE_PARTS:
@@ -615,20 +623,20 @@
     anywhere, vmem = pl.BlockSpec(memory_space=pl.ANY), pl.BlockSpec(memory_space=pltpu.VMEM)
     out = pl.pallas_call(
         functools.partial(mixer_kernel, refl, blocks),
-        in_specs=[
-            pl.BlockSpec(memory_space=pltpu.SMEM),
-            anywhere, anywhere, anywhere, anywhere, anywhere, vmem, anywhere,
-        ],
+        in_specs=[anywhere] * 8,
         out_specs=vmem,
         out_shape=pltpu.VMEM((chunk, model), bf16),
         scratch_shapes=[
+            pltpu.SMEM(prompt_lengths.shape, jnp.int32),
             pltpu.VMEM((steps, tokens, wide_step), bf16),
             pltpu.VMEM((steps, tokens, refl, wide_step), bf16),
             pltpu.VMEM((steps, tokens, refl, wide_step), bf16),
             pltpu.VMEM(beta.shape, f32),
             pltpu.VMEM(gate.shape, f32),
+            pltpu.VMEM((1, width), f32),
             dma((steps, 3)),
-            pltpu.VMEM((blocks, 2, heads, sub), f32),
+            pltpu.SemaphoreType.REGULAR,
+            pltpu.VMEM((blocks, 3, heads, sub), f32),
             pltpu.VMEM((blocks, heads, sub), f32),
             pltpu.VMEM((steps, tokens * refl, wide_step), bf16),
             pltpu.VMEM((heads, blocks, sub, 2 * width), bf16),
@@ -638,7 +646,7 @@
             pltpu.VMEM((heads, width, width), f32),
             pltpu.VMEM((heads, width, width), f32),
             pltpu.VMEM(out_weight.shape, bf16),
-            dma((3,)),
+            dma((5,)),
             *[pltpu.VMEM((heads, width, width), bf16)] * 3,
             pltpu.VMEM((2 * heads, width, width), bf16),
             pltpu.VMEM((heads, width, width), bf16),

time: 32.5 us -> 31.3 us (0.963)
  Pallas kernels: 31.6 us -> 30.2 us
    pallas_call x1, Pallas kernels: 31.6 us -> 30.2 us  [body(): pl.pallas_call(functools.partial(mixer_kernel, refl, blocks), in_specs=[a...]
where the time goes in v5:
time: 31.3 us; the launch traced here: 31 us
  Pallas kernels  30.2 us (96%)
  local copies, waits for them, and re-layouts  0.8 us (3%)
    pallas_call x1, Pallas kernels, body(): pl.pallas_call(functools.partial(mixer_kernel, refl, blocks), in_specs=[a...  30.2 us
    unnamed x1, local copies, waits for them, and re-layouts  0.8 us

profile of v5, /device:TPU:16, one launch (start us, length us, event | category | flops | bytes accessed | tf_op | source)
XLA Modules:
  0.0 31.0 jit_solution(15584482120617443595)
XLA Ops:
  0.0 30.2 %shard_map.82 = bf16[128,2048]{1,0:T(8,128)(2,1)S(1)} custom-call(s32[1,6]{1,0:T(1,128)} %len_hbm.1, bf16[256,1024]{1,0:T(8,128)(2,1)} %bitcast.14, bf16[256,2,1024]{2,1,0:T(2,128)(2,1)} %bitcast.12, bf16[256,2,1024]{2,1,0:T(2,128)(2,1)} %bitcast.13, f32[2,8,256]{2,1,0:T(8,128)} %bitcast.15, f32[8,256]{1,0:T(8,128)} %bitcast.16, f32[1,128]{1,0:T(1,128)} %bitcast.17, ...), custom_call_target="tpu_custom_call" | custom-call | tf_op jit(solution)/shard_map/pallas_call | solution.py:624
  30.2 0.8 %copy.10 = bf16[1,128,2048]{2,1,0:T(8,128)(2,1)} copy(bf16[1,128,2048]{2,1,0:T(8,128)(2,1)S(1)} %bitcast.11) | data formatting | bytes 1048576

commit v6 on v5

--- a/solution.py
+++ b/solution.py
@@ -97,21 +97,43 @@
         rows = slab_rows(rep_here, parts_here, j)
         return remote(
             weight_hbm.at[rows, pl.ds(0, shared)], peer_ref.at[rows],
-            x_send.at[j], x_recv.at[j], {"head": 1 - head_here},
+            x_send, x_recv.at[j], {"head": 1 - head_here},
         )
 
     def over_parts(j, parts):
         rows = slab_rows(rep_here, parts, j)
         return remote(
-            peer_ref.at[rows], peer_ref.at[rows], y_send.at[j], y_recv.at[j], {"parts": 1 - parts_here}
+            peer_ref.at[rows], peer_ref.at[rows], y_send, y_recv.at[j], {"parts": 1 - parts_here}
         )
 
     def over_cores(j, rep):
         parts = parts_here if j < SHARE_PARTS else 1 - parts_here
         rows = slab_rows(rep, parts, j % SHARE_PARTS)
         return remote(
-            peer_ref.at[rows], peer_ref.at[rows], core_send.at[j], core_recv.at[j], {"rep": 1 - rep_here}
+            peer_ref.at[rows], peer_ref.at[rows], core_send, core_recv, {"rep": 1 - rep_here}
         )
+
+    def quarter_rows(rep, parts, count=1):
+        return pl.ds(pl.multiple_of((rep * 2 + parts) * quarter, quarter), count * quarter)
+
+    def all_x():
+        rows = quarter_rows(rep_here, parts_here)
+        return remote(
+            weight_hbm.at[rows, pl.ds(0, shared)], peer_ref.at[rows],
+            x_send, x_recv.at[0], {"head": 1 - head_here},
+        )
+
+    def all_y():
+        rows = quarter_rows(rep_here, parts_here)
+        return remote(peer_ref.at[rows], peer_ref.at[rows], y_send, y_recv.at[0], {"parts": 1 - parts_here})
+
+    def all_cores(rep):
+        rows = quarter_rows(rep, 0, 2)
+        return remote(peer_ref.at[rows], peer_ref.at[rows], core_send, core_recv, {"rep": 1 - rep_here})
+
+    def all_normed():
+        rows = pl.ds(pl.multiple_of(others[0] * chunk, chunk), chunk)
+        return remote(normed_ref.at[rows], rows_in, norm_send, norm_recv, {"head": 1 - head_here})
 
     def relay(j):
         from_head(j).wait_recv()
@@ -123,7 +145,7 @@
         rows = pl.ds(pl.multiple_of(others[0] * chunk, chunk), chunk)
         return remote(
             normed_ref.at[rows, span], rows_in.at[:, span],
-            norm_send.at[h], norm_recv.at[h], {"head": 1 - head_here},
+            norm_send, norm_recv, {"head": 1 - head_here},
         )
 
     barrier = pltpu.get_barrier_semaphore()
@@ -240,18 +262,16 @@
     following = {"seq": lax.rem(seq_here + 1, seq_count)}
     beside = {"seq": jnp.where(last, seq_count - 2, seq_here + 1)}
     spare = jnp.where(last, heads, 0)
+    arrival = lambda h: jnp.where(last, heads, h)
 
     def send_own(h):
-        return remote(own_out.at[h], own_in.at[h + spare], own_send.at[h], own_recv.at[h + spare], beside)
+        return remote(own_out.at[h], own_in.at[h + spare], own_send, own_recv.at[arrival(h)], beside)
 
     def take_own(h):
-        return remote(own_out.at[h], own_in.at[h], own_send.at[h], own_recv.at[h], following)
-
-    def take_spare(h):
-        return remote(own_out.at[h], own_in.at[heads + h], own_send.at[h], own_recv.at[heads + h], following)
+        return remote(own_out.at[h], own_in.at[h], own_send, own_recv.at[h], following)
 
     def send_full(h):
-        return remote(full_out.at[h], full_in.at[h], full_send.at[h], full_recv.at[h], following)
+        return remote(full_out.at[h], full_in.at[h], full_send, full_recv.at[h], following)
 
     def pass_on(h, state):
         both = jnp.concatenate(split(map_ref[h]), axis=1)
@@ -538,7 +558,7 @@
                 pltpu.make_async_remote_copy(
                     src_ref=part_out.at[slot, :, part],
                     dst_ref=part_in.at[slot, :, part],
-                    send_sem=part_send.at[slot, p],
+                    send_sem=part_send.at[slot],
                     recv_sem=part_recv.at[slot, p],
                     device_id={"head": other},
                     device_id_type=MESH,
@@ -557,10 +577,8 @@
         for p in range(shared // piece):
             part = pl.ds(p * piece, piece)
             own_ref[:, part] = mm(rows, weight_ref[:, part])
-        for j in range(2 * SHARE_PARTS):
-            over_cores(j, 1 - rep_here).wait_recv()
-        for h in range(heads):
-            send_normed(h).wait_recv()
+        all_cores(1 - rep_here).wait_recv()
+        all_normed().wait_recv()
         for p in range(shared // piece):
             part = pl.ds(p * piece, piece)
             peer = mm(rows_in[...], peer_ref[:, part])
@@ -574,16 +592,15 @@
             copies[slot * pieces + p].wait_recv()
             total += part_in[slot, :, part].astype(f32)
         out_ref[:, spot] = total.astype(bf16)
-    for copy in copies:
-        copy.wait_send()
+    for slot, other in enumerate(others):
+        remote(
+            part_out.at[slot], part_in.at[slot], part_send.at[slot], part_recv.at[slot, 0], {"head": other}
+        ).wait_send()
     if shared:
-        for j in range(SHARE_PARTS):
-            from_head(j).wait_send()
-            over_parts(j, parts_here).wait_send()
-        for j in range(2 * SHARE_PARTS):
-            over_cores(j, rep_here).wait_send()
-        for h in range(heads):
-            send_normed(h).wait_send()
+        all_x().wait_send()
+        all_y().wait_send()
+        all_cores(rep_here).wait_send()
+        all_normed().wait_send()
 
     @pl.when((seq_here > 1) & (last | (not direct)))
     def _():
@@ -592,16 +609,13 @@
 
     @pl.when(seq_here == seq_count - 2)
     def _():
-        for h in range(heads):
-            take_spare(h).wait_recv()
-
-    for h in range(heads):
-        send_own(h).wait_send()
+        remote(own_out, own_in.at[pl.ds(heads, heads)], own_send, own_recv.at[heads], following).wait_recv()
+
+    remote(own_out, own_in.at[pl.ds(0, heads)], own_send, own_recv.at[0], following).wait_send()
 
     @pl.when(inner)
     def _():
-        for h in range(heads):
-            send_full(h).wait_send()
+        remote(full_out, full_in, full_send, full_recv.at[0], following).wait_send()
 
 
 def body(queries, reflect_keys, reflect_values, reflect_beta, log_decay, prompt_lengths, norm_gain, out_weight):
@@ -654,11 +668,10 @@
             pltpu.VMEM((chunk, model), f32),
             pltpu.VMEM((slots, chunk, rest), bf16),
             pltpu.VMEM((slots, chunk, rest), bf16),
-            dma((heads,)), dma((2 * heads,)), dma((heads,)), dma((heads,)), dma((slots, pieces)), dma((slots, pieces)),
+            dma, dma((heads + 1,)), dma, dma((heads,)), dma((slots,)), dma((slots, pieces)),
             pltpu.VMEM(peer_shape, bf16),
             pltpu.VMEM((chunk, wide), bf16),
-            dma((SHARE_PARTS,)), dma((SHARE_PARTS,)), dma((SHARE_PARTS,)), dma((SHARE_PARTS,)),
-            dma((2 * SHARE_PARTS,)), dma((2 * SHARE_PARTS,)), dma((heads,)), dma((heads,)),
+            dma, dma((SHARE_PARTS,)), dma, dma((SHARE_PARTS,)), dma, dma, dma, dma,
         ],
         compiler_params=pltpu.CompilerParams(
             collective_id=0, has_side_effects=True, vmem_limit_bytes=56 * 2**20

time: 31.3 us -> 30.5 us (0.974)
  Pallas kernels: 30.2 us -> 29.4 us
    pallas_call x1, Pallas kernels: 30.2 us -> 29.4 us  [body(): pl.pallas_call(functools.partial(mixer_kernel, refl, blocks), in_specs=[a...]
where the time goes in v6:
time: 30.5 us; the launch traced here: 30.2 us
  Pallas kernels  29.4 us (96%)
  local copies, waits for them, and re-layouts  0.8 us (3%)
    pallas_call x1, Pallas kernels, body(): pl.pallas_call(functools.partial(mixer_kernel, refl, blocks), in_specs=[a...  29.4 us
    unnamed x1, local copies, waits for them, and re-layouts  0.8 us

profile of v6, /device:TPU:16, one launch (start us, length us, event | category | flops | bytes accessed | tf_op | source)
XLA Modules:
  0.0 30.2 jit_solution(17719777536379281596)
XLA Ops:
  0.0 29.4 %shard_map.82 = bf16[128,2048]{1,0:T(8,128)(2,1)S(1)} custom-call(s32[1,6]{1,0:T(1,128)} %len_hbm.1, bf16[256,1024]{1,0:T(8,128)(2,1)} %bitcast.14, bf16[256,2,1024]{2,1,0:T(2,128)(2,1)} %bitcast.12, bf16[256,2,1024]{2,1,0:T(2,128)(2,1)} %bitcast.13, f32[2,8,256]{2,1,0:T(8,128)} %bitcast.15, f32[8,256]{1,0:T(8,128)} %bitcast.16, f32[1,128]{1,0:T(1,128)} %bitcast.17, ...), custom_call_target="tpu_custom_call" | custom-call | tf_op jit(solution)/shard_map/pallas_call | solution.py:638
  29.4 0.8 %copy.10 = bf16[1,128,2048]{2,1,0:T(8,128)(2,1)} copy(bf16[1,128,2048]{2,1,0:T(8,128)(2,1)S(1)} %bitcast.11) | data formatting | bytes 1048576

commit v7 on v6

--- a/solution.py
+++ b/solution.py
@@ -14,7 +14,9 @@
 PIECE = 256
 SHARE = 63
 SHARE_PARTS = 8
-RELAYS = (1, 3, 5, 6, 7)
+SWAP = 2
+ORDER = (0, 1, 2, 6, 3, 7, 4, 5)
+RELAYS = (1, 3, 5, 7, 8)
 TEAM = 2
 MESH = pl.DeviceIdType.MESH
 
@@ -59,7 +61,8 @@
 
 
 def sharing():
-    return all(lax.axis_size(name) == 2 for name in ("head", "parts", "rep"))
+    pairs = all(lax.axis_size(name) == 2 for name in ("head", "parts", "rep"))
+    return pairs and lax.axis_size("seq") % 2 == 0
 
 
 def mixer_kernel(
@@ -68,7 +71,7 @@
     rows_ref, scale_ref, kflat_ref, wrote_ref, prefix_ref, oloc_ref, read_ref, add_ref, map_ref,
     weight_ref, weight_sem, state_in, own_out, full_out, own_in, full_in, normed_ref, own_ref, part_out, part_in,
     own_send, own_recv, full_send, full_recv, part_send, part_recv,
-    peer_ref, rows_in, x_send, x_recv, y_send, y_recv, core_send, core_recv, norm_send, norm_recv,
+    peer_ref, rows_in, x_send, x_recv, y_send, y_recv, z_send, z_recv, core_send, core_recv, norm_send, norm_recv,
 ):
     heads, width = add_ref.shape[:2]
     steps = heads // HEADS_STEP
@@ -85,8 +88,22 @@
     quarter = peer_ref.shape[0] // 4
     slab = quarter // SHARE_PARTS
 
+    odd = lax.rem(seq_here, 2)
+    twin = {"seq": seq_here + 1 - 2 * odd}
+    direct_slots = SHARE_PARTS - SWAP
+
     def slab_rows(rep, parts, j):
+        if j < SWAP:
+            j = odd * SWAP + j
+        elif j < direct_slots:
+            j = j + SWAP
+        else:
+            j = (1 - odd) * SWAP + j - direct_slots
         return pl.ds(pl.multiple_of((rep * 2 + parts) * quarter + j * slab, slab), slab)
+
+    def to_twin(k, slot):
+        rows = slab_rows(rep_here, parts_here, slot)
+        return remote(peer_ref.at[rows], peer_ref.at[rows], z_send, z_recv.at[k], twin)
 
     def remote(src, dst, send, recv, device):
         return pltpu.make_async_remote_copy(
@@ -117,7 +134,7 @@
         return pl.ds(pl.multiple_of((rep * 2 + parts) * quarter, quarter), count * quarter)
 
     def all_x():
-        rows = quarter_rows(rep_here, parts_here)
+        rows = pl.ds(pl.multiple_of((rep_here * 2 + parts_here) * quarter, quarter), direct_slots * slab)
         return remote(
             weight_hbm.at[rows, pl.ds(0, shared)], peer_ref.at[rows],
             x_send, x_recv.at[0], {"head": 1 - head_here},
@@ -135,8 +152,18 @@
         rows = pl.ds(pl.multiple_of(others[0] * chunk, chunk), chunk)
         return remote(normed_ref.at[rows], rows_in, norm_send, norm_recv, {"head": 1 - head_here})
 
-    def relay(j):
-        from_head(j).wait_recv()
+    def all_z():
+        rows = pl.ds(pl.multiple_of((rep_here * 2 + parts_here) * quarter, quarter), SWAP * slab)
+        return remote(peer_ref.at[rows], peer_ref.at[rows], z_send, z_recv.at[0], twin)
+
+    def relay(place):
+        j = ORDER[place]
+        if j < direct_slots:
+            from_head(j).wait_recv()
+        else:
+            to_twin(j - direct_slots, j).wait_recv()
+        if j < SWAP:
+            to_twin(j, j).start()
         over_parts(j, parts_here).start()
         over_cores(j, rep_here).start()
 
@@ -158,7 +185,7 @@
         pl.semaphore_signal(barrier, inc=1, device_id={"head": other}, device_id_type=MESH)
     if shared:
         pl.semaphore_signal(barrier, inc=1, device_id={"parts": 1 - parts_here}, device_id_type=MESH)
-        pl.semaphore_signal(barrier, inc=1, device_id={"rep": 1 - rep_here}, device_id_type=MESH)
+    pl.semaphore_signal(barrier, inc=1, device_id={"rep": 1 - rep_here}, device_id_type=MESH)
 
     def load(s, kind):
         span = pl.ds(pl.multiple_of(s * wide, wide), wide)
@@ -182,9 +209,9 @@
         load(s, 2).start()
     load_gain.start()
     load_weight.start()
-    pl.semaphore_wait(barrier, jnp.where(first, 0, 1) + head_count - 1 + (2 if shared else 0))
+    pl.semaphore_wait(barrier, jnp.where(first, 0, 1) + head_count + (1 if shared else 0))
     if shared:
-        for j in range(SHARE_PARTS):
+        for j in range(direct_slots):
             from_head(j).start()
 
     @pl.when(seq_here > 0)
@@ -260,12 +287,13 @@
     direct = reach <= 1
     inner = (seq_here > 0) & (seq_here < seq_count - 1)
     following = {"seq": lax.rem(seq_here + 1, seq_count)}
-    beside = {"seq": jnp.where(last, seq_count - 2, seq_here + 1)}
-    spare = jnp.where(last, heads, 0)
-    arrival = lambda h: jnp.where(last, heads, h)
+    back = seq_here >= (seq_count - 2 if direct and seq_count > 2 else seq_count - 1)
+    beside = {"seq": jnp.where(back, seq_here, seq_here + 1), "rep": jnp.where(back, 1 - rep_here, rep_here)}
+    spare = jnp.where(back, heads, 0)
 
     def send_own(h):
-        return remote(own_out.at[h], own_in.at[h + spare], own_send, own_recv.at[arrival(h)], beside)
+        arrival = own_recv.at[jnp.where(back, heads, h)]
+        return remote(own_out.at[h], own_in.at[h + spare], own_send, arrival, beside)
 
     def take_own(h):
         return remote(own_out.at[h], own_in.at[h], own_send, own_recv.at[h], following)
@@ -496,56 +524,61 @@
             read_ref[s * HEADS_STEP + h, toks(b), :] = back
         return carry
 
-    lax.fori_loop(0, steps, reads_step, 0)
-    if shared:
-        while relayed < RELAYS[3]:
-            relay(relayed)
-            relayed += 1
+    def relay_until(count):
+        nonlocal relayed
+        if shared:
+            while relayed < count:
+                relay(relayed)
+                relayed += 1
+
+    def finish_heads(start, stop):
+        for g in range(start, stop, FINISH_GROUP):
+            finish_group(g, stop)
+
+    def finish_group(g, stop):
+        group = range(g, min(g + FINISH_GROUP, stop))
+
+        for h in group:
+            @pl.when(last & (seq_here == 1))
+            def _():
+                take_own(h).wait_recv()
+
+            @pl.when((seq_here > 1) & (direct | last))
+            def _():
+                send_full(h).wait_recv()
+
+            @pl.when(seq_here == 1)
+            def _():
+                state_in[h] = own_in[h]
+
+            @pl.when(seq_here > 1)
+            def _():
+                state_in[h] = full_in[h]
+
+        for h in group:
+            out = oloc_ref[h] + mm(read_ref[h], state_in[h])
+            scale = lax.rsqrt(jnp.mean(out * out, axis=-1, keepdims=True) + epsilon)
+            normed_ref[:, cols(h)] = (out * scale * gain_ref[...]).astype(bf16)
+
+        if shared:
+            for h in group:
+                send_normed(h).start()
+
+    load_gain.wait()
+    for s in range(steps - 1):
+        reads_step(s, 0)
+        finish_heads(s * HEADS_STEP, (s + 1) * HEADS_STEP)
+    relay_until(RELAYS[3])
 
     @pl.when(inner)
     def _():
         for h in range(done, heads):
             forward(h)
 
-    if shared:
-        while relayed < RELAYS[4]:
-            relay(relayed)
-            relayed += 1
-
-    load_gain.wait()
-    for g in range(0, heads, FINISH_GROUP):
-        if shared and g >= done:
-            while relayed < SHARE_PARTS:
-                relay(relayed)
-                relayed += 1
-        group = range(g, min(g + FINISH_GROUP, heads))
-
-        for h in group:
-            @pl.when(last & (seq_here == 1))
-            def _():
-                take_own(h).wait_recv()
-
-            @pl.when((seq_here > 1) & (direct | last))
-            def _():
-                send_full(h).wait_recv()
-
-            @pl.when(seq_here == 1)
-            def _():
-                state_in[h] = own_in[h]
-
-            @pl.when(seq_here > 1)
-            def _():
-                state_in[h] = full_in[h]
-
-        for h in group:
-            out = oloc_ref[h] + mm(read_ref[h], state_in[h])
-            scale = lax.rsqrt(jnp.mean(out * out, axis=-1, keepdims=True) + epsilon)
-            normed_ref[:, cols(h)] = (out * scale * gain_ref[...]).astype(bf16)
-
-        if shared:
-            for h in group:
-                send_normed(h).start()
-
+    relay_until(RELAYS[4])
+    reads_step(steps - 1, 0)
+    relay_until(SHARE_PARTS)
+    finish_heads(done, heads)
     load_weight.wait()
     piece, pieces = PIECE, (weight_ref.shape[1] - shared) // PIECE
     copies = []
@@ -599,15 +632,18 @@
     if shared:
         all_x().wait_send()
         all_y().wait_send()
+        if SWAP:
+            all_z().wait_send()
         all_cores(rep_here).wait_send()
         all_normed().wait_send()
 
-    @pl.when((seq_here > 1) & (last | (not direct)))
-    def _():
-        for h in range(heads):
-            take_own(h).wait_recv()
-
-    @pl.when(seq_here == seq_count - 2)
+    if not direct:
+        @pl.when(seq_here > 1)
+        def _():
+            for h in range(heads):
+                take_own(h).wait_recv()
+
+    @pl.when(back)
     def _():
         remote(own_out, own_in.at[pl.ds(heads, heads)], own_send, own_recv.at[heads], following).wait_recv()
 
@@ -671,7 +707,7 @@
             dma, dma((heads + 1,)), dma, dma((heads,)), dma((slots,)), dma((slots, pieces)),
             pltpu.VMEM(peer_shape, bf16),
             pltpu.VMEM((chunk, wide), bf16),
-            dma, dma((SHARE_PARTS,)), dma, dma((SHARE_PARTS,)), dma, dma, dma, dma,
+            dma, dma((SHARE_PARTS - SWAP,)), dma, dma((SHARE_PARTS,)), dma, dma((max(SWAP, 1),)), dma, dma, dma, dma,
         ],
         compiler_params=pltpu.CompilerParams(
             collective_id=0, has_side_effects=True, vmem_limit_bytes=56 * 2**20

time: 30.5 us -> 29.1 us (0.954)
  Pallas kernels: 29.4 us -> 28.1 us
    pallas_call x1, Pallas kernels: 29.4 us -> 28.1 us  [body(): pl.pallas_call(functools.partial(mixer_kernel, refl, blocks), in_specs=[a...]
where the time goes in v7:
time: 29.1 us; the launch traced here: 28.9 us
  Pallas kernels  28.1 us (97%)
  local copies, waits for them, and re-layouts  0.8 us (3%)
    pallas_call x1, Pallas kernels, body(): pl.pallas_call(functools.partial(mixer_kernel, refl, blocks), in_specs=[a...  28.1 us
    unnamed x1, local copies, waits for them, and re-layouts  0.8 us

profile of v7, /device:TPU:16, one launch (start us, length us, event | category | flops | bytes accessed | tf_op | source)
XLA Modules:
  0.0 28.9 jit_solution(15446267741543283469)
XLA Ops:
  0.0 28.1 %shard_map.82 = bf16[128,2048]{1,0:T(8,128)(2,1)S(1)} custom-call(s32[1,6]{1,0:T(1,128)} %len_hbm.1, bf16[256,1024]{1,0:T(8,128)(2,1)} %bitcast.14, bf16[256,2,1024]{2,1,0:T(2,128)(2,1)} %bitcast.12, bf16[256,2,1024]{2,1,0:T(2,128)(2,1)} %bitcast.13, f32[2,8,256]{2,1,0:T(8,128)} %bitcast.15, f32[8,256]{1,0:T(8,128)} %bitcast.16, f32[1,128]{1,0:T(1,128)} %bitcast.17, ...), custom_call_target="tpu_custom_call" | custom-call | tf_op jit(solution)/shard_map/pallas_call | solution.py:674
  28.1 0.8 %copy.10 = bf16[1,128,2048]{2,1,0:T(8,128)(2,1)} copy(bf16[1,128,2048]{2,1,0:T(8,128)(2,1)S(1)} %bitcast.11) | data formatting | bytes 1048576
